TPU v7x, 128 devices: a whole 4x4x4 slice. The times are simulated.
128 devices in a mesh: gx: 4 (over x_lo, core), gy: 4 (over y), gz: 8 (over x_hi, z).
Axes of the slice: x: 4 (x_hi: 2, x_lo: 2; x = x_hi * 2 + x_lo), y: 4, z: 4, core: 2. Of those that a mesh axis runs over, the one named last changes fastest.
Arguments:
- inv_factor: bfloat16 [4, 4, 8, 1536, 1536], P('gx', 'gy', 'gz'), as said below
- coupling: bfloat16 [4, 4, 8, 1536, 1536], P('gx', 'gy', 'gz'), may hold values from -0.15625 to 0.15625
- stiff_gg: bfloat16 [4, 4, 8, 1536, 1536], P('gx', 'gy', 'gz'), as said below
- block_order: int32 [4, 4, 8, 12], P('gx', 'gy', 'gz'), may hold values from 0 to 11, each once within a row
Outputs:
- assembled: float32 [4, 4, 8, 1536, 1536], P('gx', 'gy', 'gz')
Inputs may be any that keep to these rules, and one draw needn't show every extreme that they name: `block_order`: each subdomain's row is a permutation of 0 to 11. `stiff_gg`: each subdomain's block is symmetric. `inv_factor`: each subdomain's block is lower triangular with a positive diagonal.
All inputs are finite; a program needn't handle non-finite values.
Results may differ from a plain program's by a relative error of at most 0.0016.
Values sent between devices are 32-bit elements; how exact they have to be, the bound alone decides.
No kernel may reach another device: no remote copies, remote signals or barrier semaphores. Data moves between devices by JAX's collectives and lax.ppermute only.
A program may use at most 128 MiB of HBM per device.

v0:
```python
import jax
import jax.numpy as jnp
from jax import lax
from jax.sharding import PartitionSpec as P

BLK = 128
NBLK = 12


west_blocks = (0,)
east_blocks = (1,)
south_blocks = (2, 8, 10)
north_blocks = (3, 9, 11)
bottom_blocks = (4, 5, 8, 9)
top_blocks = (6, 7, 10, 11)


def extended(array, sides, width):
    for axis, dim in sides:
        size, length = (lax.axis_size(axis), array.shape[dim])
        up = [(i, (i + 1) % size) for i in range(size - 1)]
        down = [(j, i) for i, j in up]
        last = lax.slice_in_dim(array, length - width, length, axis=dim)
        leading = lax.slice_in_dim(array, 0, width, axis=dim)
        before = lax.ppermute(last, axis, up)
        after = lax.ppermute(leading, axis, down)
        array = jnp.concatenate([before, array, after], axis=dim)
    return array


def pair_list(listed):
    count = len(listed)
    return [(first, second) for first in range(count) for second in range(count)]


def cut_piece(tile, row_block, col_block):
    return tile[row_block * BLK : (row_block + 1) * BLK, col_block * BLK : (col_block + 1) * BLK]


def add_piece(tile, row_block, col_block, piece):
    return tile.at[
        row_block * BLK : (row_block + 1) * BLK, col_block * BLK : (col_block + 1) * BLK
    ].add(piece)


def outgoing(tile, listed):
    return jnp.stack(
        [cut_piece(tile, listed[first], listed[second]) for first, second in pair_list(listed)]
    )


def absorb(tile, listed, received):
    for number, (first, second) in enumerate(pair_list(listed)):
        row_block = listed[first]
        col_block = listed[second]
        tile = add_piece(tile, row_block, col_block, received[number])
    return tile


def section_x(tile):
    message = jnp.stack([outgoing(tile, west_blocks), outgoing(tile, east_blocks)])
    padded = extended(message, (("gx", 0),), 1)
    tile = absorb(tile, west_blocks, padded[0])
    return absorb(tile, east_blocks, padded[3])


def section_y(tile):
    message = jnp.stack([outgoing(tile, south_blocks), outgoing(tile, north_blocks)])
    padded = extended(message, (("gy", 0),), 1)
    tile = absorb(tile, south_blocks, padded[0])
    return absorb(tile, north_blocks, padded[3])


def section_z(tile):
    message = jnp.stack([outgoing(tile, bottom_blocks), outgoing(tile, top_blocks)])
    padded = extended(message, (("gz", 0),), 1)
    tile = absorb(tile, bottom_blocks, padded[0])
    return absorb(tile, top_blocks, padded[3])


def shards(inv_factor, coupling, stiff_gg, block_order):
    ranking = block_order.reshape(NBLK)
    inverse = inv_factor[0, 0, 0]
    rows_inner = inverse.shape[0]
    coupled = coupling[0, 0, 0].reshape(rows_inner, NBLK, BLK)
    coupled = jnp.take(coupled, ranking, axis=1).reshape(rows_inner, NBLK * BLK)
    stiffness = stiff_gg[0, 0, 0].reshape(NBLK, BLK, NBLK, BLK)
    stiffness = jnp.take(jnp.take(stiffness, ranking, axis=0), ranking, axis=2).reshape(
        NBLK * BLK, NBLK * BLK
    )
    weighted = jnp.dot(inverse, coupled, preferred_element_type=jnp.float32).astype(jnp.bfloat16)
    product = lax.dot_general(
        weighted, weighted, (((0,), (0,)), ((), ())), preferred_element_type=jnp.float32
    )
    tile = stiffness.astype(jnp.float32) - product
    tile = section_x(tile)
    tile = section_z(section_y(tile))
    positions = jnp.arange(NBLK, dtype=jnp.int32)
    inverse_rank = jnp.sum(
        jnp.where(ranking[None, :] == positions[:, None], positions[None, :], 0), axis=1
    )
    blocked = tile.reshape(NBLK, BLK, NBLK, BLK)
    own = jnp.take(jnp.take(blocked, inverse_rank, axis=0), inverse_rank, axis=2)
    return own.reshape(1, 1, 1, NBLK * BLK, NBLK * BLK)


def solution(mesh):
    return jax.shard_map(
        shards,
        mesh=mesh,
        in_specs=(
            P("gx", "gy", "gz", None, None),
            P("gx", "gy", "gz", None, None),
            P("gx", "gy", "gz", None, None),
            P("gx", "gy", "gz", None),
        ),
        out_specs=P("gx", "gy", "gz", None, None),
        check_vma=False,
    )
```

profile of v0, /device:TPU:21, one launch (start us, length us, event | category | flops | bytes accessed | tf_op | source)
XLA Modules:
  0.0 335.0 jit_solution(14998306717359770815)
XLA Ops:
  2.1 9.4 %reshape_squeeze.6 = bf16[12,128,12,128]{3,2,1,0:T(8,128)(2,1)} reshape(bf16[1,1,1,1536,1536]{4,3,2,1,0:T(8,128)(2,1)} %param.110) | data formatting | bytes 9437184 | tf_op jit(solution)/shard_map/reshape;squeeze | solution.py:87
  11.5 6.3 %copy.17 = bf16[12,128,12,128]{3,1,2,0:T(8,128)(2,1)} copy(bf16[12,128,12,128]{3,2,1,0:T(8,128)(2,1)} %reshape_squeeze.6) | data formatting | bytes 9437184 | tf_op jit(solution)/shard_map/reshape;squeeze | solution.py:87
  17.9 5.8 %gather_fusion = bf16[12,128,12,128]{3,1,2,0:T(8,128)(2,1)} fusion(bf16[12,128,12,128]{3,1,2,0:T(8,128)(2,1)} %copy.17, s32[1024]{0:T(1024)S(1)} %get-tuple-element.680), kind=kCustom, calls=%fused_computation | custom fusion | bytes 9437232 | tf_op jit(solution)/shard_map/jit(_take)/gather | solution.py:88
  23.7 5.0 %broadcast_select_fusion.2 = bf16[12,128,12,128]{3,1,2,0:T(8,128)(2,1)} fusion(bf16[12,128,12,128]{3,1,2,0:T(8,128)(2,1)} %gather_fusion, pred[12]{0:T(512)(128)(4,1)S(1)} %compare_and_fusion), kind=kLoop, calls=%fused_computation.12 | loop fusion | flops 2359296 | bytes 9437196 | tf_op jit(solution)/shard_map/jit(_take)/select_n | solution.py:88
  28.8 5.8 %gather_fusion.1 = bf16[12,12,128,128]{3,2,1,0:T(8,128)(2,1)} fusion(bf16[12,128,12,128]{3,1,2,0:T(8,128)(2,1)} %broadcast_select_fusion.2, s32[1024]{0:T(1024)S(1)} %get-tuple-element.680), kind=kCustom, calls=%fused_computation.1 | custom fusion | bytes 9437232 | tf_op jit(solution)/shard_map/jit(_take)/gather | solution.py:88
  34.6 8.7 %copy.18 = bf16[12,128,12,128]{3,2,1,0:T(8,128)(2,1)} copy(bf16[12,128,12,128]{3,1,0,2:T(8,128)(2,1)} %bitcast.541) | data formatting | bytes 9437184 | tf_op jit(solution)/shard_map/jit(_take)/gather | solution.py:88
  43.3 6.6 %copy.19 = bf16[1,1,1,1536,1536]{3,4,2,1,0:T(8,128)(2,1)} copy(bf16[1,1,1,1536,1536]{4,3,2,1,0:T(8,128)(2,1)} %param.109) | data formatting | bytes 9437184 | tf_op args[1]
  49.9 6.6 %copy.20 = bf16[1536,12,128]{2,0,1:T(8,128)(2,1)} copy(bf16[1536,12,128]{0,2,1:T(8,128)(2,1)} %bitcast.542) | data formatting | bytes 9437184 | tf_op jit(solution)/shard_map/reshape;squeeze | solution.py:85
  56.5 5.8 %gather_fusion.2 = bf16[12,1536,128]{2,1,0:T(8,128)(2,1)} fusion(bf16[1536,12,128]{2,0,1:T(8,128)(2,1)} %copy.20, s32[1024]{0:T(1024)S(1)} %get-tuple-element.680), kind=kCustom, calls=%fused_computation.2 | custom fusion | bytes 9437232 | tf_op jit(solution)/shard_map/jit(_take)/gather | solution.py:86
  62.4 5.0 %select_bitcast_fusion = bf16[1536,12,128]{2,0,1:T(8,128)(2,1)} fusion(bf16[12,1536,128]{2,1,0:T(8,128)(2,1)} %gather_fusion.2, pred[12]{0:T(512)(128)(4,1)S(1)} %compare_and_fusion), kind=kLoop, calls=%fused_computation.9 | loop fusion | flops 2359296 | bytes 9437196 | tf_op jit(solution)/shard_map/jit(_take)/select_n | solution.py:86
  67.4 6.8 %copy.21 = bf16[1536,12,128]{0,2,1:T(8,128)(2,1)} copy(bf16[1536,12,128]{2,0,1:T(8,128)(2,1)} %select_bitcast_fusion) | data formatting | bytes 9437184 | tf_op jit(solution)/shard_map/jit(_take)/select_n | solution.py:86
  74.2 11.0 %convolution_convert_fusion = bf16[1536,1536]{1,0:T(8,128)(2,1)S(1)} fusion(bf16[1536,1536]{0,1:T(8,128)(2,1)} %bitcast.546, bf16[1,1,1,1536,1536]{4,3,2,1,0:T(8,128)(2,1)} %param.108), kind=kOutput, calls=%fused_computation.6 | convolution fusion | flops 7250116608 | bytes 14155776 | tf_op jit(solution)/shard_map/dot_general | solution.py:91
  85.2 11.5 %convert_subtract_fusion = f32[1536,1536]{1,0:T(8,128)} fusion(bf16[1536,1536]{1,0:T(8,128)(2,1)S(1)} %convolution_convert_fusion, bf16[192,8,12,128]{3,2,1,0:T(8,128)(2,1)S(1)} %bitcast.545, pred[1536]{0:T(1024)(128)(4,1)S(1)} %broadcast_bitcast_fusion), kind=kOutput, calls=%fused_computation.5 | convolution fusion | flops 7254835200 | bytes 18875904 | tf_op jit(solution)/shard_map/dot_general | solution.py:92
  97.6 3.4 %collective-permute-start = (f32[1,1,128,128]{3,2,1,0:T(8,128)S(1)}, f32[1,1,128,128]{3,2,1,0:T(8,128)S(1)}, u32[]{:S(2)}, u32[]{:S(2)}) collective-permute-start(f32[1,1,128,128]{3,2,1,0:T(8,128)S(1)} %slice_bitcast_fusion.97), channel_id=1, source_target_pairs={{0,32},{32,64},{64,96},{1,33},{33,65},{65,97},{2,34},{34,66},{66,9... | collective-permute-start | bytes 196616 | tf_op jit(solution)/shard_map/ppermute | solution.py:25
  102.3 1.5 slice_bitcast_fusion.98
  103.8 1.9 collective-permute-start.1
  105.7 4.3 %collective-permute-done.1 = f32[1,1,128,128]{3,2,1,0:T(8,128)S(1)} collective-permute-done((f32[1,1,128,128]{3,2,1,0:T(8,128)S(1)}, f32[1,1,128,128]{3,2,1,0:T(8,128)S(1)}, u32[]{:S(2)}, u32[]{:S(2)}) %collective-permute-start.1) | collective-permute-done | bytes 65568 | tf_op jit(solution)/shard_map/ppermute | solution.py:26
  119.5 2.9 collective-permute-start.2
  122.4 2.4 collective-permute-start.3
  124.8 9.4 %collective-permute-done.2 = f32[1,9,128,128]{3,2,1,0:T(8,128)S(1)} collective-permute-done((f32[1,9,128,128]{3,2,1,0:T(8,128)S(1)}, f32[1,9,128,128]{3,2,1,0:T(8,128)S(1)}, u32[]{:S(2)}, u32[]{:S(2)}) %collective-permute-start.2) | collective-permute-done | bytes 589856 | tf_op jit(solution)/shard_map/ppermute | solution.py:25
  175.0 3.5 %collective-permute-start.4 = (f32[1,16,128,128]{3,2,1,0:T(8,128)S(1)}, f32[1,16,128,128]{3,2,1,0:T(8,128)S(1)}, u32[]{:S(2)}, u32[]{:S(2)}) collective-permute-start(f32[1,16,128,128]{3,2,1,0:T(8,128)S(1)} %bitcast.550), channel_id=1, source_target_pairs={{0,1},{1,2},{2,3},{3,4},{4,5},{5,6},{6,7},{8,9},{9,10},{10,11},{11... | collective-permute-start | bytes 3145736 | tf_op jit(solution)/shard_map/ppermute | solution.py:25
  178.6 5.4 %collective-permute-start.5 = (f32[1,16,128,128]{3,2,1,0:T(8,128)S(1)}, f32[1,16,128,128]{3,2,1,0:T(8,128)S(1)}, u32[]{:S(2)}, u32[]{:S(2)}) collective-permute-start(f32[1,16,128,128]{3,2,1,0:T(8,128)S(1)} %bitcast.549), channel_id=1, source_target_pairs={{1,0},{2,1},{3,2},{4,3},{5,4},{6,5},{7,6},{9,8},{10,9},{11,10},{12... | collective-permute-start | bytes 3145736 | tf_op jit(solution)/shard_map/ppermute | solution.py:26
  184.0 19.7 %collective-permute-done.4 = f32[1,16,128,128]{3,2,1,0:T(8,128)S(1)} collective-permute-done((f32[1,16,128,128]{3,2,1,0:T(8,128)S(1)}, f32[1,16,128,128]{3,2,1,0:T(8,128)S(1)}, u32[]{:S(2)}, u32[]{:S(2)}) %collective-permute-start.4) | collective-permute-done | bytes 1048608 | tf_op jit(solution)/shard_map/ppermute | solution.py:25
  227.3 1.5 fusion.32
  251.0 11.6 %reshape.1905 = f32[12,128,12,128]{3,2,1,0:T(8,128)} reshape(f32[1536,1536]{1,0:T(8,128)} %fusion.2) | data formatting | bytes 18874368 | tf_op jit(solution)/shard_map/reshape | solution.py:102
  262.6 11.2 %copy.22 = f32[12,128,12,128]{3,1,2,0:T(8,128)} copy(f32[12,128,12,128]{3,2,1,0:T(8,128)} %reshape.1905) | data formatting | bytes 18874368 | tf_op jit(solution)/shard_map/reshape | solution.py:102
  273.7 8.5 %gather_fusion.3 = f32[12,128,12,128]{3,1,2,0:T(8,128)} fusion(f32[12,128,12,128]{3,1,2,0:T(8,128)} %copy.22, s32[1024]{0:T(1024)S(1)} %get-tuple-element.679), kind=kCustom, calls=%fused_computation.3 | custom fusion | bytes 18874416 | tf_op jit(solution)/shard_map/jit(_take)/gather | solution.py:103
  282.2 9.5 %broadcast_select_fusion.1 = f32[12,128,12,128]{3,1,2,0:T(8,128)} fusion(f32[12,128,12,128]{3,1,2,0:T(8,128)} %gather_fusion.3, pred[12]{0:T(512)(128)(4,1)S(1)} %compare_and_fusion.1), kind=kLoop, calls=%fused_computation.11 | loop fusion | flops 2359296 | bytes 18874380 | tf_op jit(solution)/shard_map/jit(_take)/select_n | solution.py:103
  291.7 8.4 %gather_fusion.4 = f32[12,12,128,128]{3,2,1,0:T(8,128)} fusion(f32[12,128,12,128]{3,1,2,0:T(8,128)} %broadcast_select_fusion.1, s32[1024]{0:T(1024)S(1)} %get-tuple-element.679), kind=kCustom, calls=%fused_computation.4 | custom fusion | bytes 18874416 | tf_op jit(solution)/shard_map/jit(_take)/gather | solution.py:103
  300.1 14.4 %copy.23 = f32[12,128,12,128]{3,2,1,0:T(8,128)} copy(f32[12,128,12,128]{3,1,0,2:T(8,128)} %bitcast.540) | data formatting | bytes 18874368 | tf_op jit(solution)/shard_map/jit(_take)/gather | solution.py:103
  314.6 11.9 %gather.30 = f32[1,1,1,1536,1536]{4,3,2,1,0:T(8,128)} reshape(f32[12,128,12,128]{3,2,1,0:T(8,128)} %copy.23) | data formatting | bytes 18874368 | tf_op jit(solution)/shard_map/jit(_take)/gather | solution.py:103
  326.4 8.6 %broadcast_select_fusion = f32[1,1,1,1536,1536]{4,3,2,1,0:T(8,128)} fusion(f32[1,1,1,1536,1536]{4,3,2,1,0:T(8,128)} %gather.30, pred[1536]{0:T(1024)(128)(4,1)S(1)} %broadcast_bitcast_fusion.1), kind=kLoop, calls=%fused_computation.10 | loop fusion | flops 2359296 | bytes 18875904 | tf_op jit(solution)/shard_map/jit(_take)/select_n | solution.py:103
  (94 shorter events, 100.5 us)
Async XLA Ops:
  67.4 17.8 %slice-start = ((s8[6291456]{0:T(1024)(128)(4,1)}), s8[2097152]{0:T(1024)(128)(4,1)S(1)}, s32[]{:S(2)}) async-start(s8[6291456]{0:T(1024)(128)(4,1)} %bitcast.543), calls=%async_computation | async-start | bytes 4194304
  74.2 11.0 %slice-start.1 = ((s8[6291456]{0:T(1024)(128)(4,1)}), s8[4194304]{0:T(1024)(128)(4,1)S(1)}, s32[]{:S(2)}) async-start(s8[6291456]{0:T(1024)(128)(4,1)} %bitcast.543), calls=%async_computation.1 | async-start | bytes 8388608
  97.6 4.7 %collective-permute-start = (f32[1,1,128,128]{3,2,1,0:T(8,128)S(1)}, f32[1,1,128,128]{3,2,1,0:T(8,128)S(1)}, u32[]{:S(2)}, u32[]{:S(2)}) collective-permute-start(f32[1,1,128,128]{3,2,1,0:T(8,128)S(1)} %slice_bitcast_fusion.97), channel_id=1, source_target_pairs={{0,32},{32,64},{64,96},{1,33},{33,65},{65,97},{2,34},{34,66},{66,9... | collective-permute-start | bytes 196616 | tf_op jit(solution)/shard_map/ppermute | solution.py:25
  103.8 6.2 %collective-permute-start.1 = (f32[1,1,128,128]{3,2,1,0:T(8,128)S(1)}, f32[1,1,128,128]{3,2,1,0:T(8,128)S(1)}, u32[]{:S(2)}, u32[]{:S(2)}) collective-permute-start(f32[1,1,128,128]{3,2,1,0:T(8,128)S(1)} %get-tuple-element.677), channel_id=1, source_target_pairs={{32,0},{64,32},{96,64},{33,1},{65,33},{97,65},{34,2},{66,34},{98,6... | collective-permute-start | bytes 196616 | tf_op jit(solution)/shard_map/ppermute | solution.py:26
  119.5 14.7 %collective-permute-start.2 = (f32[1,9,128,128]{3,2,1,0:T(8,128)S(1)}, f32[1,9,128,128]{3,2,1,0:T(8,128)S(1)}, u32[]{:S(2)}, u32[]{:S(2)}) collective-permute-start(f32[1,9,128,128]{3,2,1,0:T(8,128)S(1)} %bitcast.548), channel_id=1, source_target_pairs={{0,8},{8,16},{16,24},{1,9},{9,17},{17,25},{2,10},{10,18},{18,26},{... | collective-permute-start | bytes 1769480 | tf_op jit(solution)/shard_map/ppermute | solution.py:25
  122.4 25.1 %collective-permute-start.3 = (f32[1,9,128,128]{3,2,1,0:T(8,128)S(1)}, f32[1,9,128,128]{3,2,1,0:T(8,128)S(1)}, u32[]{:S(2)}, u32[]{:S(2)}) collective-permute-start(f32[1,9,128,128]{3,2,1,0:T(8,128)S(1)} %bitcast.547), channel_id=1, source_target_pairs={{8,0},{16,8},{24,16},{9,1},{17,9},{25,17},{10,2},{18,10},{26,18},{... | collective-permute-start | bytes 1769480 | tf_op jit(solution)/shard_map/ppermute | solution.py:26
  175.0 28.7 %collective-permute-start.4 = (f32[1,16,128,128]{3,2,1,0:T(8,128)S(1)}, f32[1,16,128,128]{3,2,1,0:T(8,128)S(1)}, u32[]{:S(2)}, u32[]{:S(2)}) collective-permute-start(f32[1,16,128,128]{3,2,1,0:T(8,128)S(1)} %bitcast.550), channel_id=1, source_target_pairs={{0,1},{1,2},{2,3},{3,4},{4,5},{5,6},{6,7},{8,9},{9,10},{10,11},{11... | collective-permute-start | bytes 3145736 | tf_op jit(solution)/shard_map/ppermute | solution.py:25
  178.6 48.7 %collective-permute-start.5 = (f32[1,16,128,128]{3,2,1,0:T(8,128)S(1)}, f32[1,16,128,128]{3,2,1,0:T(8,128)S(1)}, u32[]{:S(2)}, u32[]{:S(2)}) collective-permute-start(f32[1,16,128,128]{3,2,1,0:T(8,128)S(1)} %bitcast.549), channel_id=1, source_target_pairs={{1,0},{2,1},{3,2},{4,3},{5,4},{6,5},{7,6},{9,8},{10,9},{11,10},{12... | collective-permute-start | bytes 3145736 | tf_op jit(solution)/shard_map/ppermute | solution.py:26
where the time goes:
time: 342 us; the launch traced here: 335 us
  local copies, waits for them, and re-layouts  152 us (44%)
  other arithmetic  107 us (31%)
  waiting for transfers between devices  34.6 us (10%)
  matrix products  22.5 us (7%)
  starting transfers between devices  19.5 us (6%)
    scatter-add x50, other arithmetic, add_piece(): return tile.at[row_block * BLK:(row_block + 1) * BLK, col_block * BLK:(co...  74 us
    gather x3, local copies, waits for them, and re-layouts, shards(): jnp.take(jnp.take(blocked, inverse_rank, axis=0), inverse_rank, axis=2)  34.7 us
    ppermute x3, waiting for transfers between devices, extended(): before = lax.ppermute(last, axis, up)  30.3 us
    unnamed x28, local copies, waits for them, and re-layouts  27 us
    reshape x2, local copies, waits for them, and re-layouts, shards(): blocked = tile.reshape(NBLK, BLK, NBLK, BLK)  22.7 us
    another operation x2, local copies, waits for them, and re-layouts, shards(): stiffness = stiff_gg[0, 0, 0].reshape(NBLK, BLK, NBLK, BLK)  15.7 us
    gather x2, local copies, waits for them, and re-layouts, shards(): jnp.take(jnp.take(stiffness, ranking, axis=0), ranking, axis=2)  14.5 us
    dot_general x1, matrix products, shards(): lax.dot_general(weighted, weighted, (((0,), (0,)), ((), ())), preferred_e...  11.5 us
  transfers between devices with their start and end apart: 6, of which 4 were waited for; matrix products, arithmetic and copies ran while one was open for 11% of the time, Pallas kernels for 0%

commit v1 on v0

v1 whole, which is shorter than its diff:
```python
import functools

import jax
import jax.numpy as jnp
from jax import lax
from jax.experimental import pallas as pl
from jax.experimental.pallas import tpu as pltpu
from jax.sharding import PartitionSpec as P

BLK = 128
NBLK = 12
PAN = 256

FIRST = (4, 5, 8, 9, 6, 7, 10, 11)
SECOND = (2, 3, 0, 1)
PAIRS = {"A": (4, 5), "B": (8, 9), "C": (6, 7), "D": (10, 11), "E": (2, 3), "F": (0, 1)}
BOTTOM = (4, 5, 8, 9)
TOP = (6, 7, 10, 11)
SOUTH = (2, 8, 10)
NORTH = (3, 9, 11)
REST = ("AC", "AD", "BC", "EA", "EC", "FA", "FB", "FC", "FD", "FE")


def upper(listed):
    return [(k, l) for i, k in enumerate(listed) for l in listed[i:]]


Z_LOW, Z_HIGH = upper(BOTTOM), upper(TOP)
Y_LOW, Y_HIGH = upper(SOUTH), upper(NORTH)
MIXED = ("EE", "EB", "ED", "BD", "FF")


def block_start(order, k):
    return pl.multiple_of(order[k] * BLK, BLK)


def stiff_copy(order, stiff, buf, sem, slot, k, l):
    return pltpu.make_async_copy(
        stiff.at[pl.ds(block_start(order, k), BLK), pl.ds(block_start(order, l), BLK)],
        buf.at[slot],
        sem,
    )


def column_copies(order, coupling, buf, sems, listed):
    copies = []
    for pan in range(buf.shape[0] // PAN):
        rows = pl.ds(pan * PAN, PAN)
        copies.append(
            [
                pltpu.make_async_copy(
                    coupling.at[rows, pl.ds(block_start(order, k), BLK)],
                    buf.at[rows, pl.ds(at * BLK, BLK)],
                    sems.at[pan],
                )
                for at, k in enumerate(listed)
            ]
        )
    return copies


def factor_copies(inverse, buf, sems):
    return [
        pltpu.make_async_copy(
            inverse.at[pl.ds(pan * PAN, PAN), pl.ds(0, (pan + 1) * PAN)],
            buf.at[pl.ds(pan * PAN, PAN), pl.ds(0, (pan + 1) * PAN)],
            sems.at[pan],
        )
        for pan in range(inverse.shape[0] // PAN)
    ]


def weigh(inverse, coupled, pan):
    depth = (pan + 1) * PAN
    return jnp.dot(
        inverse[pan * PAN : depth, :depth], coupled[:depth, :], preferred_element_type=jnp.float32
    ).astype(jnp.bfloat16)


def gram(left, right):
    return lax.dot_general(left, right, (((0,), (0,)), ((), ())), preferred_element_type=jnp.float32)


def first_kernel(order, inverse, coupling, stiff, zd, zu, w1, lbuf, cbuf, sbuf, lsem, csem, ssem):
    lcopies = factor_copies(inverse, lbuf, lsem)
    ccopies = column_copies(order, coupling, cbuf, csem, FIRST)
    for lcopy, group in zip(lcopies, ccopies):
        lcopy.start()
        for copy in group:
            copy.start()
    blocks = Z_LOW + Z_HIGH
    scopies = [stiff_copy(order, stiff, sbuf, ssem, i, k, l) for i, (k, l) in enumerate(blocks)]
    for copy in scopies:
        copy.start()
    for pan, (lcopy, group) in enumerate(zip(lcopies, ccopies)):
        lcopy.wait()
        for copy in group:
            copy.wait()
        w1[pan * PAN : (pan + 1) * PAN, :] = weigh(lbuf, cbuf, pan)
    for copy in scopies:
        copy.wait()
    for base, out, listed, half in ((0, zd, BOTTOM, 0), (10, zu, TOP, 512)):
        pairs = upper(listed)
        first = gram(w1[:, half : half + 256], w1[:, half : half + 512])
        second = gram(w1[:, half + 256 : half + 512], w1[:, half + 256 : half + 512])
        for n, (k, l) in enumerate(pairs):
            i, j = listed.index(k), listed.index(l)
            source, row, col = (first, i, j) if i < 2 else (second, i - 2, j - 2)
            out[n] = sbuf[base + n].astype(jnp.float32) - source[
                row * BLK : (row + 1) * BLK, col * BLK : (col + 1) * BLK
            ]


def second_kernel(order, inverse, coupling, stiff, w1, zd, zu, yd, yu, xd, xu, w2, keep, lbuf, cbuf, sbuf, lsem, csem, ssem):
    lcopies = factor_copies(inverse, lbuf, lsem)
    ccopies = column_copies(order, coupling, cbuf, csem, SECOND)
    for lcopy, group in zip(lcopies, ccopies):
        lcopy.start()
        for copy in group:
            copy.start()
    blocks = [(k, l) for name in MIXED for k, l in cells(name)]
    scopies = [stiff_copy(order, stiff, sbuf, ssem, i, k, l) for i, (k, l) in enumerate(blocks)]
    for copy in scopies:
        copy.start()
    for pan, (lcopy, group) in enumerate(zip(lcopies, ccopies)):
        lcopy.wait()
        for copy in group:
            copy.wait()
        w2[pan * PAN : (pan + 1) * PAN, :] = weigh(lbuf, cbuf, pan)
    for copy in scopies:
        copy.wait()
    yd[Y_LOW.index((8, 8))] = zd[Z_LOW.index((8, 8))]
    yd[Y_LOW.index((10, 10))] = zu[Z_HIGH.index((10, 10))]
    yu[Y_HIGH.index((9, 9))] = zd[Z_LOW.index((9, 9))]
    yu[Y_HIGH.index((11, 11))] = zu[Z_HIGH.index((11, 11))]
    targets = {}
    for n, pair in enumerate(Y_LOW):
        targets[pair] = (yd, n)
    for n, pair in enumerate(Y_HIGH):
        targets[pair] = (yu, n)
    targets[(0, 0)], targets[(1, 1)] = (xd, 0), (xu, 0)
    at = kept = 0
    for name in MIXED:
        result = gram(part(name[0], w1, w2), part(name[1], w1, w2))
        rows, cols = PAIRS[name[0]], PAIRS[name[1]]
        for k, l in cells(name):
            row, col = rows.index(k), cols.index(l)
            value = sbuf[at].astype(jnp.float32) - result[
                row * BLK : (row + 1) * BLK, col * BLK : (col + 1) * BLK
            ]
            at += 1
            if (k, l) in targets:
                out, slot = targets[(k, l)]
                out[slot] = value
            else:
                keep[kept] = value
                kept += 1


def cells(name):
    rows, cols = PAIRS[name[0]], PAIRS[name[1]]
    return [(k, l) for k in rows for l in cols if name[0] != name[1] or k <= l]


def part(letter, w1, w2):
    if letter in "ABCD":
        at = "ABCD".index(letter) * 256
        return w1[:, at : at + 256]
    at = "EF".index(letter) * 256
    return w2[:, at : at + 256]


SHARED = set(Z_LOW + Z_HIGH + Y_LOW + Y_HIGH + [(0, 0), (1, 1)])
KEPT = [cell for name in MIXED for cell in cells(name) if cell not in SHARED]


def put(order, out, stage, sem, slot, k, l):
    copy = pltpu.make_async_copy(
        stage.at[slot],
        out.at[pl.ds(block_start(order, k), BLK), pl.ds(block_start(order, l), BLK)],
        sem,
    )
    copy.start()
    return copy


def rest_kernel(order, stiff, w1, w2, keep, out, sbuf, stage, ssem, osem):
    blocks = [(k, l) for name in REST for k, l in cells(name)]
    scopies = [stiff_copy(order, stiff, sbuf, ssem, i, k, l) for i, (k, l) in enumerate(blocks)]
    for copy in scopies:
        copy.start()
    copies = []

    def emit(k, l, value):
        slot = len(copies)
        stage[slot] = value
        copies.append(put(order, out, stage, osem, slot, k, l))
        stage[slot + 1] = value.T
        copies.append(put(order, out, stage, osem, slot + 1, l, k))

    for n, (k, l) in enumerate(KEPT):
        emit(k, l, keep[n])
    for copy in scopies:
        copy.wait()
    at = 0
    for name in REST:
        result = gram(part(name[0], w1, w2), part(name[1], w1, w2))
        rows, cols = PAIRS[name[0]], PAIRS[name[1]]
        for k, l in cells(name):
            row, col = rows.index(k), cols.index(l)
            emit(
                k,
                l,
                sbuf[at].astype(jnp.float32)
                - result[row * BLK : (row + 1) * BLK, col * BLK : (col + 1) * BLK],
            )
            at += 1
    for copy in copies:
        copy.wait()


def last_kernel(order, zd, zu, yd, yu, xd, xu, fzl, fzh, fyl, fyh, fxl, fxh, cll, clh, chl, chh, before, out, stage, osem):
    copies = []

    def emit(k, l, value):
        slot = len(copies)
        stage[slot] = value
        copies.append(put(order, out, stage, osem, slot, k, l))
        if k != l:
            stage[slot + 1] = value.T
            copies.append(put(order, out, stage, osem, slot + 1, l, k))

    edges = {8: (fyl, Y_HIGH.index((9, 9)), cll), 9: (fyh, Y_LOW.index((8, 8)), chl)}
    edges[10] = (fyl, Y_HIGH.index((11, 11)), clh)
    edges[11] = (fyh, Y_LOW.index((10, 10)), chh)
    emit(0, 0, xd[0] + fxl[0])
    emit(1, 1, xu[0] + fxh[0])
    for pairs, own, other in ((Y_LOW, yd, fyl), (Y_HIGH, yu, fyh)):
        for n, (k, l) in enumerate(pairs):
            if k != l or k in (2, 3):
                emit(k, l, own[n] + other[n])
    for pairs, own, other in ((Z_LOW, zd, fzl), (Z_HIGH, zu, fzh)):
        for n, (k, l) in enumerate(pairs):
            value = own[n] + other[n]
            if k == l and k in edges:
                across, slot, corner = edges[k]
                value = value + across[slot] + corner[0]
            emit(k, l, value)
    for copy in copies:
        copy.wait()


def shifts(axis):
    size = lax.axis_size(axis)
    return [(i, i + 1) for i in range(size - 1)]


def swap(pairs):
    return [(j, i) for i, j in pairs]


HBM = pl.BlockSpec(memory_space=pltpu.HBM)
VMEM = pl.BlockSpec(memory_space=pltpu.VMEM)
SMEM = pl.BlockSpec(memory_space=pltpu.SMEM)
MB = 1024 * 1024


def shape(*dims, dtype=jnp.float32):
    return jax.ShapeDtypeStruct(dims, dtype)


def params(limit):
    return pltpu.CompilerParams(vmem_limit_bytes=limit * MB)


def shards(inv_factor, coupling, stiff_gg, block_order):
    rows = inv_factor.shape[3]
    order = block_order.reshape(NBLK)
    inverse = inv_factor.reshape(rows, rows)
    coupled = coupling.reshape(rows, NBLK * BLK)
    stiff = stiff_gg.reshape(NBLK * BLK, NBLK * BLK)
    panels = rows // PAN
    dma = pltpu.SemaphoreType.DMA
    zd, zu, w1 = pl.pallas_call(
        first_kernel,
        out_shape=(shape(10, BLK, BLK), shape(10, BLK, BLK), shape(rows, 1024, dtype=jnp.bfloat16)),
        in_specs=[SMEM, HBM, HBM, HBM],
        out_specs=(VMEM, VMEM, VMEM),
        scratch_shapes=[
            pltpu.VMEM((rows, rows), jnp.bfloat16),
            pltpu.VMEM((rows, 1024), jnp.bfloat16),
            pltpu.VMEM((20, BLK, BLK), jnp.bfloat16),
            dma((panels,)),
            dma((panels,)),
            dma,
        ],
        compiler_params=params(30),
        cost_estimate=pl.CostEstimate(flops=6 * 10**9, bytes_accessed=8 * 10**6, transcendentals=0),
        name="first",
    )(order, inverse, coupled, stiff)
    up, down = shifts("gz"), swap(shifts("gz"))
    fzl = lax.ppermute(zu, "gz", up)
    fzh = lax.ppermute(zd, "gz", down)
    mixed = sum(len(cells(name)) for name in MIXED)
    yd, yu, xd, xu, w2, keep = pl.pallas_call(
        second_kernel,
        out_shape=(
            shape(6, BLK, BLK),
            shape(6, BLK, BLK),
            shape(1, BLK, BLK),
            shape(1, BLK, BLK),
            shape(rows, 512, dtype=jnp.bfloat16),
            shape(len(KEPT), BLK, BLK),
        ),
        in_specs=[SMEM, HBM, HBM, HBM, VMEM, VMEM, VMEM],
        out_specs=(VMEM,) * 6,
        scratch_shapes=[
            pltpu.VMEM((rows, rows), jnp.bfloat16),
            pltpu.VMEM((rows, 512), jnp.bfloat16),
            pltpu.VMEM((mixed, BLK, BLK), jnp.bfloat16),
            dma((panels,)),
            dma((panels,)),
            dma,
        ],
        compiler_params=params(30),
        cost_estimate=pl.CostEstimate(flops=4 * 10**9, bytes_accessed=8 * 10**6, transcendentals=0),
        name="second",
    )(order, inverse, coupled, stiff, w1, zd, zu)
    sy, ny = shifts("gy"), swap(shifts("gy"))
    fyl = lax.ppermute(yu, "gy", sy)
    fyh = lax.ppermute(yd, "gy", ny)
    size = lax.axis_size("gz")

    def corner(block, ypairs, zpairs):
        pairs = [(a * size + c, b * size + d) for a, b in ypairs for c, d in zpairs]
        return lax.ppermute(block, ("gy", "gz"), pairs)

    cll = corner(zu[9:10], sy, up)
    clh = corner(zd[9:10], sy, down)
    chl = corner(zu[7:8], ny, up)
    chh = corner(zd[7:8], ny, down)
    fxl = lax.ppermute(xu, "gx", shifts("gx"))
    fxh = lax.ppermute(xd, "gx", swap(shifts("gx")))
    out = pl.pallas_call(
        rest_kernel,
        out_shape=shape(NBLK * BLK, NBLK * BLK),
        in_specs=[SMEM, HBM, VMEM, VMEM, VMEM],
        out_specs=HBM,
        scratch_shapes=[
            pltpu.VMEM((40, BLK, BLK), jnp.bfloat16),
            pltpu.VMEM((96, BLK, BLK), jnp.float32),
            dma,
            dma,
        ],
        compiler_params=params(30),
        cost_estimate=pl.CostEstimate(flops=2 * 10**9, bytes_accessed=8 * 10**6, transcendentals=0),
        name="rest",
    )(order, stiff, w1, w2, keep)
    out = pl.pallas_call(
        last_kernel,
        out_shape=shape(NBLK * BLK, NBLK * BLK),
        in_specs=[SMEM] + [VMEM] * 16 + [HBM],
        out_specs=HBM,
        scratch_shapes=[pltpu.VMEM((48, BLK, BLK), jnp.float32), dma],
        input_output_aliases={17: 0},
        compiler_params=params(20),
        cost_estimate=pl.CostEstimate(flops=10**6, bytes_accessed=8 * 10**6, transcendentals=0),
        name="last",
    )(order, zd, zu, yd, yu, xd, xu, fzl, fzh, fyl, fyh, fxl, fxh, cll, clh, chl, chh, out)
    return out.reshape(1, 1, 1, NBLK * BLK, NBLK * BLK)


def solution(mesh):
    return jax.shard_map(
        shards,
        mesh=mesh,
        in_specs=(
            P("gx", "gy", "gz", None, None),
            P("gx", "gy", "gz", None, None),
            P("gx", "gy", "gz", None, None),
            P("gx", "gy", "gz", None),
        ),
        out_specs=P("gx", "gy", "gz", None, None),
        check_vma=False,
    )
```

time: 342 us -> 80.4 us (0.24); the launches traced: 335 us -> 79.9 us
  local copies, waits for them, and re-layouts: 152 us -> 7.69 us
  other arithmetic: 107 us -> 0 us
  matrix products: 22.5 us -> 0 us
  Pallas kernels: 0 us -> 21.5 us
  waiting for transfers between devices: 34.6 us -> 17.6 us
  starting transfers between devices: 19.5 us -> 32.8 us
    scatter-add x50 -> x0, other arithmetic: 74 us -> none  [add_piece(): return tile.at[row_block * BLK:(row_block + 1) * BLK, col_block * BLK:(co...]
    gather x8 -> x0, local copies, waits for them, and re-layouts: 69.4 us -> none  [the longest x3 34.7 us: shards(): jnp.take(jnp.take(blocked, inverse_rank, axis=0), inverse_rank, axis=2)]
    select_n x6 -> x0, other arithmetic: 28.8 us -> none  [the longest x1 9.49 us: shards(): jnp.take(blocked, inverse_rank, axis=0)]
    another operation x7 -> x0, local copies, waits for them, and re-layouts: 25 us -> none  [the longest x2 15.7 us: shards(): stiffness = stiff_gg[0, 0, 0].reshape(NBLK, BLK, NBLK, BLK)]
    reshape x2 -> x0, local copies, waits for them, and re-layouts: 22.7 us -> none  [shards(): blocked = tile.reshape(NBLK, BLK, NBLK, BLK)]
    dot_general x2 -> x0, matrix products: 22.5 us -> none  [the longest x1 11.5 us: shards(): lax.dot_general(weighted, weighted, (((0,), (0,)), ((), ())), preferred_e...]
    pallas_call x0 -> x4, Pallas kernels: none -> 21.5 us  [the longest x1 7.21 us: shards(): pl.pallas_call(first_kernel, out_shape=(shape(10, BLK, BLK), shape(10, BL...]
    unnamed x28 -> x10, local copies, waits for them, and re-layouts: 27 us -> 7.67 us
  transfers between devices with their start and end apart: 6 -> 10, of which waited for: 4 -> 3; matrix products, arithmetic and copies ran while one was open for 11% -> 0% of each run, Pallas kernels for 0% -> 15%
where the time goes in v1:
time: 80.4 us; the launch traced here: 79.9 us
  starting transfers between devices  32.8 us (41%)
  Pallas kernels  21.5 us (27%)
  waiting for transfers between devices  17.6 us (22%)
  local copies, waits for them, and re-layouts  7.69 us (10%)
    ppermute x4, waiting for transfers between devices, corner(): return lax.ppermute(block, ('gy', 'gz'), pairs)  13.9 us
    ppermute x4, starting transfers between devices, corner(): return lax.ppermute(block, ('gy', 'gz'), pairs)  9.91 us
    unnamed x10, local copies, waits for them, and re-layouts  7.67 us
    pallas_call x1, Pallas kernels, shards(): pl.pallas_call(first_kernel, out_shape=(shape(10, BLK, BLK), shape(10, BL...  7.21 us
    pallas_call x1, Pallas kernels, shards(): pl.pallas_call(rest_kernel, out_shape=shape(NBLK * BLK, NBLK * BLK), in_s...  6.7 us
    ppermute x1, starting transfers between devices, shards(): fxh = lax.ppermute(xd, 'gx', swap(shifts('gx')))  6.56 us
    ppermute x1, starting transfers between devices, shards(): fzh = lax.ppermute(zd, 'gz', down)  5.59 us
    pallas_call x1, Pallas kernels, shards(): pl.pallas_call(second_kernel, out_shape=(shape(6, BLK, BLK), shape(6, BLK...  5.35 us
  transfers between devices with their start and end apart: 10, of which 3 were waited for; matrix products, arithmetic and copies ran while one was open for 0% of the time, Pallas kernels for 15%

profile of v1, /device:TPU:21, one launch (start us, length us, event | category | flops | bytes accessed | tf_op | source)
XLA Modules:
  0.0 79.9 jit_solution(3754822873809948567)
XLA Ops:
  0.0 0.0 copy-start
  0.0 2.3 %copy-done = bf16[1,1,1,1536,1536]{4,3,2,1,0:T(8,128)(2,1)S(1)} copy-done((bf16[1,1,1,1536,1536]{4,3,2,1,0:T(8,128)(2,1)S(1)}, bf16[1,1,1,1536,1536]{4,3,2,1,0:T(8,128)(2,1)}, u32[]{:S(2)}) %copy-start) | copy-done | bytes 4718616
  2.3 0.0 copy-start.2
  2.3 2.3 %copy-done.2 = bf16[1,1,1,1536,1536]{4,3,2,1,0:T(8,128)(2,1)S(1)} copy-done((bf16[1,1,1,1536,1536]{4,3,2,1,0:T(8,128)(2,1)S(1)}, bf16[1,1,1,1536,1536]{4,3,2,1,0:T(8,128)(2,1)}, u32[]{:S(2)}) %copy-start.2) | copy-done | bytes 4718616
  4.7 2.3 %copy-done.3 = bf16[1,1,1,1536,1536]{4,3,2,1,0:T(8,128)(2,1)S(1)} copy-done((bf16[1,1,1,1536,1536]{4,3,2,1,0:T(8,128)(2,1)S(1)}, bf16[1,1,1,1536,1536]{4,3,2,1,0:T(8,128)(2,1)}, u32[]{:S(2)}) %copy-start.3) | copy-done | bytes 4718616
  7.0 0.7 copy-done.4
  7.7 7.2 %first.1 = (f32[10,128,128]{2,1,0:T(8,128)S(1)}, f32[10,128,128]{2,1,0:T(8,128)S(1)}, bf16[1536,1024]{1,0:T(8,128)(2,1)S(1)}) custom-call(s32[12]{0:T(128)S(1)} %bitcast.12, bf16[1536,1536]{1,0:T(8,128)(2,1)S(1)} %bitcast.8, bf16[1536,1536]{1,0:T(8,128)(2,1)S(1)} %bitcast.10, bf16[1536,1536]{1,0:T(8,128)(2,1)S(1)} %bitcast.5), custom_call_target="tpu_custom_call" | custom-call | flops 6000000000 | bytes 8000000 | tf_op jit(solution)/shard_map/first/pallas_call | solution.py:284
  14.9 5.6 %collective-permute-start.1 = (f32[10,128,128]{2,1,0:T(8,128)S(1)}, f32[10,128,128]{2,1,0:T(8,128)S(1)}, u32[]{:S(2)}, u32[]{:S(2)}) collective-permute-start(f32[10,128,128]{2,1,0:T(8,128)S(1)} %get-tuple-element.14.zd), channel_id=1, source_target_pairs={{1,0},{2,1},{3,2},{4,3},{5,4},{6,5},{7,6},{9,8},{10,9},{11,10},{12... | collective-permute-start | bytes 1966088 | tf_op jit(solution)/shard_map/ppermute | solution.py:303
  20.5 1.9 %collective-permute-start.9 = (f32[1,128,128]{2,1,0:T(8,128)S(1)}, f32[1,128,128]{2,1,0:T(8,128)S(1)}, u32[]{:S(2)}, u32[]{:S(2)}) collective-permute-start(f32[1,128,128]{2,1,0:T(8,128)S(1)} %get-tuple-element.23), channel_id=1, source_target_pairs={{9,0},{10,1},{11,2},{12,3},{13,4},{14,5},{15,6},{17,8},{18,9},{19,... | collective-permute-start | bytes 196616 | tf_op jit(solution)/shard_map/ppermute | solution.py:336
  22.4 2.9 %collective-permute-start.7 = (f32[1,128,128]{2,1,0:T(8,128)S(1)}, f32[1,128,128]{2,1,0:T(8,128)S(1)}, u32[]{:S(2)}, u32[]{:S(2)}) collective-permute-start(f32[1,128,128]{2,1,0:T(8,128)S(1)} %get-tuple-element.24), channel_id=1, source_target_pairs={{1,8},{2,9},{3,10},{4,11},{5,12},{6,13},{7,14},{9,16},{10,17},{11,... | collective-permute-start | bytes 196616 | tf_op jit(solution)/shard_map/ppermute | solution.py:336
  25.4 3.4 %collective-permute-start = (f32[10,128,128]{2,1,0:T(8,128)S(1)}, f32[10,128,128]{2,1,0:T(8,128)S(1)}, u32[]{:S(2)}, u32[]{:S(2)}) collective-permute-start(f32[10,128,128]{2,1,0:T(8,128)S(1)} %get-tuple-element.15.zu), channel_id=1, source_target_pairs={{0,1},{1,2},{2,3},{3,4},{4,5},{5,6},{6,7},{8,9},{9,10},{10,11},{11... | collective-permute-start | bytes 1966088 | tf_op jit(solution)/shard_map/ppermute | solution.py:302
  28.7 0.0 copy-start.1
  28.7 5.3 %second.1 = (f32[6,128,128]{2,1,0:T(8,128)S(1)}, f32[6,128,128]{2,1,0:T(8,128)S(1)}, f32[1,128,128]{2,1,0:T(8,128)S(1)}, f32[1,128,128]{2,1,0:T(8,128)S(1)}, bf1...) custom-call(s32[12]{0:T(128)S(1)} %bitcast.13, bf16[1536,1536]{1,0:T(8,128)(2,1)S(1)} %bitcast.9, ...), custom_call_target="tpu_custom_call" | custom-call | flops 4000000000 | bytes 8000000 | tf_op jit(solution)/shard_map/second/pallas_call | solution.py:305
  34.1 2.1 %collective-permute-start.3 = (f32[6,128,128]{2,1,0:T(8,128)S(1)}, f32[6,128,128]{2,1,0:T(8,128)S(1)}, u32[]{:S(2)}, u32[]{:S(2)}) collective-permute-start(f32[6,128,128]{2,1,0:T(8,128)S(1)} %get-tuple-element.17.yd), channel_id=1, source_target_pairs={{8,0},{16,8},{24,16},{9,1},{17,9},{25,17},{10,2},{18,10},{26,18},{... | collective-permute-start | bytes 1179656 | tf_op jit(solution)/shard_map/ppermute | solution.py:331
  36.2 0.0 collective-permute-done.9.chh
  36.2 3.2 %collective-permute-start.2 = (f32[6,128,128]{2,1,0:T(8,128)S(1)}, f32[6,128,128]{2,1,0:T(8,128)S(1)}, u32[]{:S(2)}, u32[]{:S(2)}) collective-permute-start(f32[6,128,128]{2,1,0:T(8,128)S(1)} %get-tuple-element.18.yu), channel_id=1, source_target_pairs={{0,8},{8,16},{16,24},{1,9},{9,17},{17,25},{2,10},{10,18},{18,26},{... | collective-permute-start | bytes 1179656 | tf_op jit(solution)/shard_map/ppermute | solution.py:330
  39.4 0.0 collective-permute-done.7.clh
  39.5 3.2 %collective-permute-start.8 = (f32[1,128,128]{2,1,0:T(8,128)S(1)}, f32[1,128,128]{2,1,0:T(8,128)S(1)}, u32[]{:S(2)}, u32[]{:S(2)}) collective-permute-start(f32[1,128,128]{2,1,0:T(8,128)S(1)} %get-tuple-element.25), channel_id=1, source_target_pairs={{8,1},{9,2},{10,3},{11,4},{12,5},{13,6},{14,7},{16,9},{17,10},{18,... | collective-permute-start | bytes 196616 | tf_op jit(solution)/shard_map/ppermute | solution.py:336
  42.6 6.3 %collective-permute-done.8.chl = f32[1,128,128]{2,1,0:T(8,128)S(1)} collective-permute-done((f32[1,128,128]{2,1,0:T(8,128)S(1)}, f32[1,128,128]{2,1,0:T(8,128)S(1)}, u32[]{:S(2)}, u32[]{:S(2)}) %collective-permute-start.8) | collective-permute-done | bytes 65568 | tf_op jit(solution)/shard_map/ppermute | solution.py:336
  49.0 1.9 %collective-permute-start.6 = (f32[1,128,128]{2,1,0:T(8,128)S(1)}, f32[1,128,128]{2,1,0:T(8,128)S(1)}, u32[]{:S(2)}, u32[]{:S(2)}) collective-permute-start(f32[1,128,128]{2,1,0:T(8,128)S(1)} %get-tuple-element.26), channel_id=1, source_target_pairs={{0,9},{1,10},{2,11},{3,12},{4,13},{5,14},{6,15},{8,17},{9,18},{10,... | collective-permute-start | bytes 196616 | tf_op jit(solution)/shard_map/ppermute | solution.py:336
  50.9 7.6 %collective-permute-done.6.cll = f32[1,128,128]{2,1,0:T(8,128)S(1)} collective-permute-done((f32[1,128,128]{2,1,0:T(8,128)S(1)}, f32[1,128,128]{2,1,0:T(8,128)S(1)}, u32[]{:S(2)}, u32[]{:S(2)}) %collective-permute-start.6) | collective-permute-done | bytes 65568 | tf_op jit(solution)/shard_map/ppermute | solution.py:336
  58.5 6.6 %collective-permute-start.5 = (f32[1,128,128]{2,1,0:T(8,128)S(1)}, f32[1,128,128]{2,1,0:T(8,128)S(1)}, u32[]{:S(2)}, u32[]{:S(2)}) collective-permute-start(f32[1,128,128]{2,1,0:T(8,128)S(1)} %get-tuple-element.19.xd), channel_id=1, source_target_pairs={{32,0},{64,32},{96,64},{33,1},{65,33},{97,65},{34,2},{66,34},{98,6... | collective-permute-start | bytes 196616 | tf_op jit(solution)/shard_map/ppermute | solution.py:343
  65.1 3.7 %collective-permute-done.5.fxh = f32[1,128,128]{2,1,0:T(8,128)S(1)} collective-permute-done((f32[1,128,128]{2,1,0:T(8,128)S(1)}, f32[1,128,128]{2,1,0:T(8,128)S(1)}, u32[]{:S(2)}, u32[]{:S(2)}) %collective-permute-start.5) | collective-permute-done | bytes 65568 | tf_op jit(solution)/shard_map/ppermute | solution.py:343
  68.7 2.1 %collective-permute-start.4 = (f32[1,128,128]{2,1,0:T(8,128)S(1)}, f32[1,128,128]{2,1,0:T(8,128)S(1)}, u32[]{:S(2)}, u32[]{:S(2)}) collective-permute-start(f32[1,128,128]{2,1,0:T(8,128)S(1)} %get-tuple-element.20.xu), channel_id=1, source_target_pairs={{0,32},{32,64},{64,96},{1,33},{33,65},{65,97},{2,34},{34,66},{66,9... | collective-permute-start | bytes 196616 | tf_op jit(solution)/shard_map/ppermute | solution.py:342
  70.8 0.0 copy-done.1
  70.8 6.7 %rest.1.before = f32[1536,1536]{1,0:T(8,128)} custom-call(s32[12]{0:T(128)S(1)} %bitcast.14, bf16[1536,1536]{1,0:T(8,128)(2,1)S(1)} %bitcast.7, bf16[1536,1024]{1,0:T(8,128)(2,1)S(1)} %get-tuple-element.16.w1, bf16[1536,512]{1,0:T(8,128)(2,1)S(1)} %get-tuple-element.21.w2, f32[8,128,128]{2,1,0:T(8,128)S(1)} %get-tuple-element.22.keep), custom_call_target="tpu_custom_call" | custom-call | flops 2000000000 | bytes 8000000 | tf_op jit(solution)/shard_map/rest/pallas_call | solution.py:344
  77.5 0.0 collective-permute-done.4.fxl
  77.5 0.0 collective-permute-done.3.fyh
  77.6 0.0 collective-permute-done.2.fyl
  77.6 0.0 collective-permute-done.1.fzh
  77.6 0.0 collective-permute-done.fzl
  77.6 2.2 %last.1 = f32[1536,1536]{1,0:T(8,128)} custom-call(s32[12]{0:T(128)S(1)} %bitcast.15, f32[10,128,128]{2,1,0:T(8,128)S(1)} %get-tuple-element.14.zd, f32[10,128,128]{2,1,0:T(8,128)S(1)} %get-tuple-element.15.zu, f32[6,128,128]{2,1,0:T(8,128)S(1)} %get-tuple-element.17.yd, f32[6,128,128]{2,1,0:T(8,128)S(1)} %get-tuple-element.18.yu, ...), custom_call_target="tpu_custom_call", output_to_operand_aliasing={{}: (17, {})} | custom-call | flops 1000000 | bytes 8000000 | tf_op jit(solution)/shard_map/last/pallas_call | solution.py:359
  (4 shorter events, 0.0 us)
Async XLA Ops:
  0.0 2.3 %copy-start = (bf16[1,1,1,1536,1536]{4,3,2,1,0:T(8,128)(2,1)S(1)}, bf16[1,1,1,1536,1536]{4,3,2,1,0:T(8,128)(2,1)}, u32[]{:S(2)}) copy-start(bf16[1,1,1,1536,1536]{4,3,2,1,0:T(8,128)(2,1)} %param.6) | copy-start | bytes 14155780
  2.3 2.3 %copy-start.2 = (bf16[1,1,1,1536,1536]{4,3,2,1,0:T(8,128)(2,1)S(1)}, bf16[1,1,1,1536,1536]{4,3,2,1,0:T(8,128)(2,1)}, u32[]{:S(2)}) copy-start(bf16[1,1,1,1536,1536]{4,3,2,1,0:T(8,128)(2,1)} %param.4) | copy-start | bytes 14155780
  4.7 2.3 %copy-start.3 = (bf16[1,1,1,1536,1536]{4,3,2,1,0:T(8,128)(2,1)S(1)}, bf16[1,1,1,1536,1536]{4,3,2,1,0:T(8,128)(2,1)}, u32[]{:S(2)}) copy-start(bf16[1,1,1,1536,1536]{4,3,2,1,0:T(8,128)(2,1)} %param.5) | copy-start | bytes 14155780
  7.0 0.7 copy-start.4
  14.9 62.7 %collective-permute-start.1 = (f32[10,128,128]{2,1,0:T(8,128)S(1)}, f32[10,128,128]{2,1,0:T(8,128)S(1)}, u32[]{:S(2)}, u32[]{:S(2)}) collective-permute-start(f32[10,128,128]{2,1,0:T(8,128)S(1)} %get-tuple-element.14.zd), channel_id=1, source_target_pairs={{1,0},{2,1},{3,2},{4,3},{5,4},{6,5},{7,6},{9,8},{10,9},{11,10},{12... | collective-permute-start | bytes 1966088 | tf_op jit(solution)/shard_map/ppermute | solution.py:303
  20.5 15.7 %collective-permute-start.9 = (f32[1,128,128]{2,1,0:T(8,128)S(1)}, f32[1,128,128]{2,1,0:T(8,128)S(1)}, u32[]{:S(2)}, u32[]{:S(2)}) collective-permute-start(f32[1,128,128]{2,1,0:T(8,128)S(1)} %get-tuple-element.23), channel_id=1, source_target_pairs={{9,0},{10,1},{11,2},{12,3},{13,4},{14,5},{15,6},{17,8},{18,9},{19,... | collective-permute-start | bytes 196616 | tf_op jit(solution)/shard_map/ppermute | solution.py:336
  22.4 17.0 %collective-permute-start.7 = (f32[1,128,128]{2,1,0:T(8,128)S(1)}, f32[1,128,128]{2,1,0:T(8,128)S(1)}, u32[]{:S(2)}, u32[]{:S(2)}) collective-permute-start(f32[1,128,128]{2,1,0:T(8,128)S(1)} %get-tuple-element.24), channel_id=1, source_target_pairs={{1,8},{2,9},{3,10},{4,11},{5,12},{6,13},{7,14},{9,16},{10,17},{11,... | collective-permute-start | bytes 196616 | tf_op jit(solution)/shard_map/ppermute | solution.py:336
  25.4 52.2 %collective-permute-start = (f32[10,128,128]{2,1,0:T(8,128)S(1)}, f32[10,128,128]{2,1,0:T(8,128)S(1)}, u32[]{:S(2)}, u32[]{:S(2)}) collective-permute-start(f32[10,128,128]{2,1,0:T(8,128)S(1)} %get-tuple-element.15.zu), channel_id=1, source_target_pairs={{0,1},{1,2},{2,3},{3,4},{4,5},{5,6},{6,7},{8,9},{9,10},{10,11},{11... | collective-permute-start | bytes 1966088 | tf_op jit(solution)/shard_map/ppermute | solution.py:302
  28.7 42.1 %copy-start.1 = (bf16[1,1,1,1536,1536]{4,3,2,1,0:T(8,128)(2,1)S(1)}, bf16[1,1,1,1536,1536]{4,3,2,1,0:T(8,128)(2,1)}, u32[]{:S(2)}) copy-start(bf16[1,1,1,1536,1536]{4,3,2,1,0:T(8,128)(2,1)} %param.6) | copy-start | bytes 14155780
  34.1 43.5 %collective-permute-start.3 = (f32[6,128,128]{2,1,0:T(8,128)S(1)}, f32[6,128,128]{2,1,0:T(8,128)S(1)}, u32[]{:S(2)}, u32[]{:S(2)}) collective-permute-start(f32[6,128,128]{2,1,0:T(8,128)S(1)} %get-tuple-element.17.yd), channel_id=1, source_target_pairs={{8,0},{16,8},{24,16},{9,1},{17,9},{25,17},{10,2},{18,10},{26,18},{... | collective-permute-start | bytes 1179656 | tf_op jit(solution)/shard_map/ppermute | solution.py:331
  36.2 41.4 %collective-permute-start.2 = (f32[6,128,128]{2,1,0:T(8,128)S(1)}, f32[6,128,128]{2,1,0:T(8,128)S(1)}, u32[]{:S(2)}, u32[]{:S(2)}) collective-permute-start(f32[6,128,128]{2,1,0:T(8,128)S(1)} %get-tuple-element.18.yu), channel_id=1, source_target_pairs={{0,8},{8,16},{16,24},{1,9},{9,17},{17,25},{2,10},{10,18},{18,26},{... | collective-permute-start | bytes 1179656 | tf_op jit(solution)/shard_map/ppermute | solution.py:330
  39.5 9.5 %collective-permute-start.8 = (f32[1,128,128]{2,1,0:T(8,128)S(1)}, f32[1,128,128]{2,1,0:T(8,128)S(1)}, u32[]{:S(2)}, u32[]{:S(2)}) collective-permute-start(f32[1,128,128]{2,1,0:T(8,128)S(1)} %get-tuple-element.25), channel_id=1, source_target_pairs={{8,1},{9,2},{10,3},{11,4},{12,5},{13,6},{14,7},{16,9},{17,10},{18,... | collective-permute-start | bytes 196616 | tf_op jit(solution)/shard_map/ppermute | solution.py:336
  49.0 9.5 %collective-permute-start.6 = (f32[1,128,128]{2,1,0:T(8,128)S(1)}, f32[1,128,128]{2,1,0:T(8,128)S(1)}, u32[]{:S(2)}, u32[]{:S(2)}) collective-permute-start(f32[1,128,128]{2,1,0:T(8,128)S(1)} %get-tuple-element.26), channel_id=1, source_target_pairs={{0,9},{1,10},{2,11},{3,12},{4,13},{5,14},{6,15},{8,17},{9,18},{10,... | collective-permute-start | bytes 196616 | tf_op jit(solution)/shard_map/ppermute | solution.py:336
  58.5 10.2 %collective-permute-start.5 = (f32[1,128,128]{2,1,0:T(8,128)S(1)}, f32[1,128,128]{2,1,0:T(8,128)S(1)}, u32[]{:S(2)}, u32[]{:S(2)}) collective-permute-start(f32[1,128,128]{2,1,0:T(8,128)S(1)} %get-tuple-element.19.xd), channel_id=1, source_target_pairs={{32,0},{64,32},{96,64},{33,1},{65,33},{97,65},{34,2},{66,34},{98,6... | collective-permute-start | bytes 196616 | tf_op jit(solution)/shard_map/ppermute | solution.py:343
  68.7 8.8 %collective-permute-start.4 = (f32[1,128,128]{2,1,0:T(8,128)S(1)}, f32[1,128,128]{2,1,0:T(8,128)S(1)}, u32[]{:S(2)}, u32[]{:S(2)}) collective-permute-start(f32[1,128,128]{2,1,0:T(8,128)S(1)} %get-tuple-element.20.xu), channel_id=1, source_target_pairs={{0,32},{32,64},{64,96},{1,33},{33,65},{65,97},{2,34},{34,66},{66,9... | collective-permute-start | bytes 196616 | tf_op jit(solution)/shard_map/ppermute | solution.py:342

commit v2 on v0

v2 whole, which is shorter than its diff:
```python
import jax
import jax.numpy as jnp
from jax import lax
from jax.experimental import pallas as pl
from jax.experimental.pallas import tpu as pltpu
from jax.sharding import PartitionSpec as P

BLK = 128
NBLK = 12
PAN = 256

PAIRS = {"A": (4, 5), "B": (8, 9), "C": (6, 7), "D": (10, 11), "E": (2, 3), "F": (0, 1)}
COLUMNS = (8, 9, 10, 11, 4, 5, 6, 7, 2, 3, 0, 1)
Z_HIGH, Z_LOW = ((6, 7), (6, 10), (6, 11), (7, 10), (7, 11), (10, 11)), ((4, 5), (4, 8), (4, 9), (5, 8), (5, 9), (8, 9))
Z_HIGH_PACK, Z_LOW_PACK = ((6, 7), (11, 10)), ((4, 5), (8, 9))
Y_HIGH, Y_LOW = ((3, 3), (3, 9), (3, 11), (9, 11)), ((2, 2), (2, 8), (2, 10), (8, 10))
KEPT = ((2, 3), (2, 9), (3, 8), (2, 11), (3, 10), (8, 11), (9, 10), (0, 1))
FACES = 8 * BLK
MESSAGE = FACES + 8


def position(order, k):
    if k < 2:
        at = k ^ (lax.axis_index("gx") % 2)
    elif k < 4:
        at = 2 + ((k - 2) ^ (lax.axis_index("gy") % 2))
    elif k < 8:
        at = 4 + ((k - 4) ^ (2 * (lax.axis_index("gz") % 2)))
    else:
        at = 8 + ((k - 8) ^ (lax.axis_index("gy") % 2 + 2 * (lax.axis_index("gz") % 2)))
    return pl.multiple_of(order[at] * BLK, BLK)


def positions(order):
    return [position(order, k) for k in range(NBLK)]


def fetch_order(order, osmem, sem):
    copy = pltpu.make_async_copy(order, osmem, sem)
    copy.start()
    return copy


def stiff_copies(at, stiff, buf, sem, blocks):
    copies = [
        pltpu.make_async_copy(
            stiff.at[pl.ds(at[k], BLK), pl.ds(at[l], BLK)], buf.at[pl.ds(n * BLK, BLK), :], sem
        )
        for n, (k, l) in enumerate(blocks)
    ]
    for copy in copies:
        copy.start()
    return copies


def weigh(lbuf, cbuf, columns, pan):
    depth = (pan + 1) * PAN
    return jnp.dot(
        lbuf[pan * PAN : depth, :depth], cbuf[:depth, columns], preferred_element_type=jnp.float32
    ).astype(jnp.bfloat16)


def gram(left, right):
    return lax.dot_general(left, right, (((0,), (0,)), ((), ())), preferred_element_type=jnp.float32)


def rows_ge():
    r = lax.broadcasted_iota(jnp.int32, (BLK, BLK), 0)
    c = lax.broadcasted_iota(jnp.int32, (BLK, BLK), 1)
    return r, c


def pack(first, second):
    r, c = rows_ge()
    return jnp.where(r <= c, first, second), jnp.sum(jnp.where(r == c, second, 0.0), axis=0, keepdims=True)


def unpack(tile, diagonal):
    r, c = rows_ge()
    turned = tile.T
    first = jnp.where(r <= c, tile, turned)
    return first, jnp.where(r > c, tile, jnp.where(r < c, turned, diagonal))


def two_rows(first, second):
    row = lax.broadcasted_iota(jnp.int32, (8, BLK), 0)
    return jnp.where(row == 0, first, jnp.where(row == 1, second, 0.0))


def piece(result, i, j):
    return result[i * BLK : (i + 1) * BLK, j * BLK : (j + 1) * BLK]


def slot(n):
    return slice(n * BLK, (n + 1) * BLK)


EDGE_BLOCKS = ((8, 8), (8, 9), (9, 9), (10, 10), (10, 11), (11, 11))


def edge_kernel(order, inverse, coupling, stiff, lbuf, cbuf, wbd, yda, ydb, zpart, osmem, sbuf, osem, lsem, csem, rsem, ssem):
    fetch = fetch_order(order, osmem, osem)
    panels = lbuf.shape[0] // PAN
    lcopies = [
        pltpu.make_async_copy(
            inverse.at[pl.ds(pan * PAN, PAN), pl.ds(0, (pan + 1) * PAN)],
            lbuf.at[pl.ds(pan * PAN, PAN), pl.ds(0, (pan + 1) * PAN)],
            lsem.at[pan],
        )
        for pan in range(panels)
    ]
    for copy in lcopies[:2]:
        copy.start()
    fetch.wait()
    at = positions(osmem)
    ccopies = []
    for pan in range(panels):
        rows = pl.ds(pan * PAN, PAN)
        group = [
            pltpu.make_async_copy(
                coupling.at[rows, pl.ds(at[k], BLK)], cbuf.at[rows, pl.ds(n * BLK, BLK)], csem.at[pan]
            )
            for n, k in enumerate(COLUMNS[:4])
        ]
        ccopies.append(group)
        if pan >= 2:
            lcopies[pan].start()
        for copy in group:
            copy.start()
    scopies = stiff_copies(at, stiff, sbuf, ssem, EDGE_BLOCKS)
    later = [
        pltpu.make_async_copy(
            coupling.at[:, pl.ds(at[k], BLK)], cbuf.at[:, pl.ds((n + 4) * BLK, BLK)], rsem
        )
        for n, k in enumerate(COLUMNS[4:])
    ]
    for copy in later:
        copy.start()
    for pan in range(panels):
        lcopies[pan].wait()
        for copy in ccopies[pan]:
            copy.wait()
        wbd[pan * PAN : (pan + 1) * PAN, :] = weigh(lbuf, cbuf, slice(0, 512), pan)
    for copy in scopies:
        copy.wait()
    full = []
    for n in range(2):
        half = wbd[:, n * 256 : (n + 1) * 256]
        result = gram(half, half)
        for m, (i, j) in enumerate(((0, 0), (0, 1), (1, 1))):
            full.append(sbuf[slot(n * 3 + m)].astype(jnp.float32) - piece(result, i, j))
    b8, b89, b9, b10, b1011, b11 = full
    ydb[:BLK], row = pack(b8, b10)
    ydb[BLK:] = two_rows(row, 0.0)
    yda[:BLK], row = pack(b11, b9)
    yda[BLK:] = two_rows(row, 0.0)
    zpart[slot(0)] = b89
    zpart[slot(1)] = b1011
    zpart[slot(2)], low = pack(b8, b9)
    zpart[slot(3)], high = pack(b11, b10)
    zpart[4 * BLK :] = two_rows(low, high)
    for copy in later:
        copy.wait()


FACE_BLOCKS = ((4, 4), (4, 5), (5, 5), (4, 8), (4, 9), (5, 8), (5, 9), (6, 6), (6, 7), (7, 7), (6, 10), (6, 11), (7, 10), (7, 11))


def face_kernel(order, stiff, lbuf, cbuf, wbd, zpart, wac, za, zb, osmem, sbuf, osem, ssem):
    fetch_order(order, osmem, osem).wait()
    at = positions(osmem)
    scopies = stiff_copies(at, stiff, sbuf, ssem, FACE_BLOCKS)
    for pan in range(lbuf.shape[0] // PAN):
        wac[pan * PAN : (pan + 1) * PAN, :] = weigh(lbuf, cbuf, slice(512, 1024), pan)
    for copy in scopies:
        copy.wait()
    for n, (out, part) in enumerate(((zb, 0), (za, 1))):
        own = wac[:, n * 256 : (n + 1) * 256]
        inner = gram(own, own)
        outer = gram(own, wbd[:, n * 256 : (n + 1) * 256])
        base = n * 7

        def value(m, result, i, j):
            return sbuf[slot(base + m)].astype(jnp.float32) - piece(result, i, j)

        out[slot(6)], row = pack(value(0, inner, 0, 0), value(2, inner, 1, 1))
        out[slot(0)] = value(1, inner, 0, 1)
        for m, (i, j) in enumerate(((0, 0), (0, 1), (1, 0), (1, 1))):
            out[slot(1 + m)] = value(3 + m, outer, i, j)
        out[slot(5)] = zpart[slot(part)]
        out[slot(7)] = zpart[slot(2 + part)]
        out[FACES:] = two_rows(row, zpart[4 * BLK + part : 4 * BLK + part + 1])


def join_kernel(za, zb, fya, fyb, za_out, zb_out):
    del za, zb
    r, c = rows_ge()
    above = r <= c
    row = lax.broadcasted_iota(jnp.int32, (8, BLK), 0) == 1
    za_out[slot(7)] = za_out[slot(7)] + jnp.where(above, fya[:BLK], fyb[:BLK])
    za_out[FACES:] = za_out[FACES:] + jnp.where(row, fyb[BLK : BLK + 1], 0.0)
    zb_out[slot(7)] = zb_out[slot(7)] + jnp.where(above, fyb[:BLK], fya[:BLK])
    zb_out[FACES:] = zb_out[FACES:] + jnp.where(row, fya[BLK : BLK + 1], 0.0)


SIDE_BLOCKS = tuple((k, l) for k in (2, 3) for l in (2, 3, 8, 9, 10, 11) if k <= l) + ((8, 10), (8, 11), (9, 10), (9, 11), (0, 0), (0, 1), (1, 1))


def side_kernel(order, stiff, lbuf, cbuf, wbd, after, wef, yea, yeb, xa, xb, keep, osmem, sbuf, osem, ssem):
    del after
    fetch_order(order, osmem, osem).wait()
    at = positions(osmem)
    scopies = stiff_copies(at, stiff, sbuf, ssem, SIDE_BLOCKS)
    for pan in range(lbuf.shape[0] // PAN):
        wef[pan * PAN : (pan + 1) * PAN, :] = weigh(lbuf, cbuf, slice(1024, 1536), pan)
    for copy in scopies:
        copy.wait()
    e, f = wef[:, :256], wef[:, 256:]
    targets = {pair: (yea, n) for n, pair in enumerate(Y_HIGH)} | {pair: (yeb, n) for n, pair in enumerate(Y_LOW)}
    targets |= {pair: (keep, n) for n, pair in enumerate(KEPT)} | {(1, 1): (xa, 0), (0, 0): (xb, 0)}

    def emit(result, rows, cols):
        for i, k in enumerate(rows):
            for j, l in enumerate(cols):
                if k <= l:
                    out, n = targets[(k, l)]
                    m = SIDE_BLOCKS.index((k, l))
                    out[slot(n)] = sbuf[slot(m)].astype(jnp.float32) - piece(result, i, j)

    emit(gram(e, e), (2, 3), (2, 3))
    emit(gram(e, wbd[...]), (2, 3), (8, 9, 10, 11))
    emit(gram(wbd[:, :256], wbd[:, 256:]), (8, 9), (10, 11))
    emit(gram(f, f), (0, 1), (0, 1))


REST = (
    ("F", (("bd", (8, 9, 10, 11)), ("ac", (4, 5, 6, 7)), ("e", (2, 3)))),
    ("E", (("ac", (4, 5, 6, 7)),)),
    ("A", (("c", (6, 7)), ("d", (10, 11)))),
    ("C", (("b", (8, 9)),)),
)
REST_BLOCKS = tuple((k, l) for left, rights in REST for _, cols in rights for k in PAIRS[left] for l in cols)


def put(at, out, stage, sem, n, k, l):
    copy = pltpu.make_async_copy(
        stage.at[pl.ds(n * BLK, BLK), :], out.at[pl.ds(at[k], BLK), pl.ds(at[l], BLK)], sem
    )
    copy.start()
    return copy


def rest_kernel(order, stiff, wbd, wac, wef, keep, out, osmem, sbuf, turned, stage, osem, ssem, wsem):
    fetch_order(order, osmem, osem).wait()
    at = positions(osmem)
    scopies = stiff_copies(at, stiff, sbuf, ssem, REST_BLOCKS)
    copies = []

    def emit(k, l, value):
        n = len(copies)
        stage[slot(n)] = value
        copies.append(put(at, out, stage, wsem, n, k, l))
        stage[slot(n + 1)] = value.T
        copies.append(put(at, out, stage, wsem, n + 1, l, k))

    whole = {"ac": (wac, 0, 512), "bd": (wbd, 0, 512), "e": (wef, 0, 256), "f": (wef, 256, 512), "a": (wac, 0, 256)}
    whole |= {"c": (wac, 256, 512), "b": (wbd, 0, 256), "d": (wbd, 256, 512)}
    for n, (k, l) in enumerate(KEPT):
        emit(k, l, keep[slot(n)])
    for copy in scopies:
        copy.wait()
    m = 0
    for left, rights in REST:
        ref, lo, hi = whole[left.lower()]
        turned[...] = ref[:, lo:hi].T
        for name, cols in rights:
            ref, lo, hi = whole[name]
            result = jnp.dot(turned[...], ref[:, lo:hi], preferred_element_type=jnp.float32)
            for i, k in enumerate(PAIRS[left]):
                for j, l in enumerate(cols):
                    emit(k, l, sbuf[slot(m)].astype(jnp.float32) - piece(result, i, j))
                    m += 1
    for copy in copies:
        copy.wait()


def last_kernel(order, za, zb, fza, fzb, yea, yeb, fyea, fyeb, xa, xb, fxa, fxb, before, out, osmem, stage, osem, wsem):
    del before
    fetch_order(order, osmem, osem).wait()
    at = positions(osmem)
    copies = []

    def emit(k, l, value):
        n = len(copies)
        stage[slot(n)] = value
        copies.append(put(at, out, stage, wsem, n, k, l))
        if k != l:
            stage[slot(n + 1)] = value.T
            copies.append(put(at, out, stage, wsem, n + 1, l, k))

    emit(0, 0, xb[...] + fxb[...])
    emit(1, 1, xa[...] + fxa[...])
    for pairs, own, other in ((Y_HIGH, yea, fyea), (Y_LOW, yeb, fyeb)):
        for n, (k, l) in enumerate(pairs):
            emit(k, l, own[slot(n)] + other[slot(n)])
    for pairs, packs, own, other in ((Z_LOW, Z_LOW_PACK, zb, fzb), (Z_HIGH, Z_HIGH_PACK, za, fza)):
        for n, (k, l) in enumerate(pairs):
            emit(k, l, own[slot(n)] + other[slot(n)])
        for n, (k, l) in enumerate(packs):
            row = slice(FACES + n, FACES + n + 1)
            first, second = unpack(own[slot(6 + n)] + other[slot(6 + n)], own[row] + other[row])
            emit(k, k, first)
            emit(l, l, second)
    for copy in copies:
        copy.wait()


def exchange(value, axis, start):
    size = lax.axis_size(axis)
    pairs = [(i, i + 1) for i in range(start, size - 1, 2)]
    return lax.ppermute(value, axis, pairs + [(j, i) for i, j in pairs])


HBM = pl.BlockSpec(memory_space=pltpu.HBM)
VMEM = pl.BlockSpec(memory_space=pltpu.VMEM)
DMA = pltpu.SemaphoreType.DMA


def shape(*dims, dtype=jnp.float32):
    return jax.ShapeDtypeStruct(dims, dtype)


def params(mib):
    return pltpu.CompilerParams(vmem_limit_bytes=mib * 1024 * 1024)


def cost(gigaflops, megabytes):
    return pl.CostEstimate(
        flops=int(gigaflops * 1e9), bytes_accessed=int(megabytes * 1e6), transcendentals=0
    )


def in_hbm(value):
    return pltpu.with_memory_space_constraint(value, pltpu.HBM)


def shards(inv_factor, coupling, stiff_gg, block_order):
    rows = inv_factor.shape[3]
    size = NBLK * BLK
    half = jnp.bfloat16
    order = in_hbm(block_order.reshape(NBLK))
    inverse = in_hbm(inv_factor.reshape(rows, rows))
    coupled = in_hbm(coupling.reshape(rows, size))
    stiff = in_hbm(stiff_gg.reshape(size, size))
    panels = rows // PAN
    osmem = pltpu.SMEM((NBLK,), jnp.int32)

    def stiff_scratch(blocks):
        return pltpu.VMEM((len(blocks) * BLK, BLK), half)

    lbuf, cbuf, wbd, yda, ydb, zpart = pl.pallas_call(
        edge_kernel,
        out_shape=(
            shape(rows, rows, dtype=half),
            shape(rows, size, dtype=half),
            shape(rows, 512, dtype=half),
            shape(BLK + 8, BLK),
            shape(BLK + 8, BLK),
            shape(4 * BLK + 8, BLK),
        ),
        in_specs=[HBM] * 4,
        out_specs=(VMEM,) * 6,
        scratch_shapes=[osmem, stiff_scratch(EDGE_BLOCKS), DMA, DMA((panels,)), DMA((panels,)), DMA, DMA],
        compiler_params=params(12),
        cost_estimate=cost(3, 8),
        name="edges",
    )(order, inverse, coupled, stiff)
    fya = exchange(yda, "gy", 0)
    fyb = exchange(ydb, "gy", 1)
    wac, za, zb = pl.pallas_call(
        face_kernel,
        out_shape=(shape(rows, 512, dtype=half), shape(MESSAGE, BLK), shape(MESSAGE, BLK)),
        in_specs=[HBM, HBM] + [VMEM] * 4,
        out_specs=(VMEM,) * 3,
        scratch_shapes=[osmem, stiff_scratch(FACE_BLOCKS), DMA, DMA],
        compiler_params=params(12),
        cost_estimate=cost(3, 1),
        name="faces",
    )(order, stiff, lbuf, cbuf, wbd, zpart)
    za, zb = pl.pallas_call(
        join_kernel,
        out_shape=(shape(MESSAGE, BLK), shape(MESSAGE, BLK)),
        in_specs=[VMEM] * 4,
        out_specs=(VMEM,) * 2,
        input_output_aliases={0: 0, 1: 1},
        compiler_params=params(2),
        cost_estimate=cost(0.1, 0.1),
        name="join",
    )(za, zb, fya, fyb)
    fzb = exchange(zb, "gz", 1)
    fza = exchange(za, "gz", 0)
    wef, yea, yeb, xa, xb, keep = pl.pallas_call(
        side_kernel,
        out_shape=(
            shape(rows, 512, dtype=half),
            shape(4 * BLK, BLK),
            shape(4 * BLK, BLK),
            shape(BLK, BLK),
            shape(BLK, BLK),
            shape(len(KEPT) * BLK, BLK),
        ),
        in_specs=[HBM, HBM] + [VMEM] * 4,
        out_specs=(VMEM,) * 6,
        scratch_shapes=[osmem, stiff_scratch(SIDE_BLOCKS), DMA, DMA],
        compiler_params=params(12),
        cost_estimate=cost(3, 1),
        name="sides",
    )(order, stiff, lbuf, cbuf, wbd, za)
    fyea = exchange(yea, "gy", 0)
    fyeb = exchange(yeb, "gy", 1)
    fxa = exchange(xa, "gx", 0)
    fxb = exchange(xb, "gx", 1)
    out = pl.pallas_call(
        rest_kernel,
        out_shape=shape(size, size),
        in_specs=[HBM, HBM] + [VMEM] * 4,
        out_specs=HBM,
        scratch_shapes=[
            osmem,
            stiff_scratch(REST_BLOCKS),
            pltpu.VMEM((PAN, rows), half),
            pltpu.VMEM((2 * (len(KEPT) + len(REST_BLOCKS)) * BLK, BLK), jnp.float32),
            DMA,
            DMA,
            DMA,
        ],
        compiler_params=params(16),
        cost_estimate=cost(3, 8),
        name="rest",
    )(order, stiff, wbd, wac, wef, keep)
    out = pl.pallas_call(
        last_kernel,
        out_shape=shape(size, size),
        in_specs=[HBM] + [VMEM] * 12 + [HBM],
        out_specs=HBM,
        scratch_shapes=[osmem, pltpu.VMEM((48 * BLK, BLK), jnp.float32), DMA, DMA],
        input_output_aliases={13: 0},
        compiler_params=params(12),
        cost_estimate=cost(0.1, 3),
        name="last",
    )(order, za, zb, fza, fzb, yea, yeb, fyea, fyeb, xa, xb, fxa, fxb, out)
    return out.reshape(1, 1, 1, size, size)


def solution(mesh):
    return jax.shard_map(
        shards,
        mesh=mesh,
        in_specs=(
            P("gx", "gy", "gz", None, None),
            P("gx", "gy", "gz", None, None),
            P("gx", "gy", "gz", None, None),
            P("gx", "gy", "gz", None),
        ),
        out_specs=P("gx", "gy", "gz", None, None),
        check_vma=False,
    )
```

time: 342 us -> 41 us (0.12); the launches traced: 335 us -> 40.3 us
  local copies, waits for them, and re-layouts: 152 us -> 0 us
  other arithmetic: 107 us -> 0 us
  waiting for transfers between devices: 34.6 us -> 0.02 us
  Pallas kernels: 0 us -> 22.8 us
  matrix products: 22.5 us -> 0 us
    scatter-add x50 -> x0, other arithmetic: 74 us -> none  [add_piece(): return tile.at[row_block * BLK:(row_block + 1) * BLK, col_block * BLK:(co...]
    gather x8 -> x0, local copies, waits for them, and re-layouts: 69.4 us -> none  [the longest x3 34.7 us: shards(): jnp.take(jnp.take(blocked, inverse_rank, axis=0), inverse_rank, axis=2)]
    ppermute x6 -> x8, waiting for transfers between devices: 34.6 us -> 0.02 us  [exchange(): return lax.ppermute(value, axis, pairs + [(j, i) for i, j in pairs])]
    select_n x6 -> x0, other arithmetic: 28.8 us -> none  [the longest x1 9.49 us: shards(): jnp.take(blocked, inverse_rank, axis=0)]
    unnamed x28 -> x0, local copies, waits for them, and re-layouts: 27 us -> none
    another operation x7 -> x0, local copies, waits for them, and re-layouts: 25 us -> none  [the longest x2 15.7 us: shards(): stiffness = stiff_gg[0, 0, 0].reshape(NBLK, BLK, NBLK, BLK)]
    pallas_call x0 -> x6, Pallas kernels: none -> 22.8 us  [the longest x1 5.95 us: shards(): pl.pallas_call(rest_kernel, out_shape=shape(size, size), in_specs=[HBM, H...]
    reshape x2 -> x0, local copies, waits for them, and re-layouts: 22.7 us -> none  [shards(): blocked = tile.reshape(NBLK, BLK, NBLK, BLK)]
  transfers between devices with their start and end apart: 6 -> 8, of which waited for: 4 -> 0; matrix products, arithmetic and copies ran while one was open for 11% -> 0% of each run, Pallas kernels for 0% -> 37%
where the time goes in v2:
time: 41 us; the launch traced here: 40.3 us
  Pallas kernels  22.8 us (56%)
  starting transfers between devices  17.3 us (42%)
    ppermute x8, starting transfers between devices, exchange(): return lax.ppermute(value, axis, pairs + [(j, i) for i, j in pairs])  17.3 us
    pallas_call x1, Pallas kernels, shards(): pl.pallas_call(rest_kernel, out_shape=shape(size, size), in_specs=[HBM, H...  5.95 us
    pallas_call x1, Pallas kernels, shards(): pl.pallas_call(edge_kernel, out_shape=(shape(rows, rows, dtype=half), sha...  5.59 us
    pallas_call x1, Pallas kernels, shards(): pl.pallas_call(side_kernel, out_shape=(shape(rows, 512, dtype=half), shap...  4.83 us
    pallas_call x1, Pallas kernels, shards(): pl.pallas_call(face_kernel, out_shape=(shape(rows, 512, dtype=half), shap...  4.08 us
    pallas_call x1, Pallas kernels, shards(): pl.pallas_call(last_kernel, out_shape=shape(size, size), in_specs=[HBM] +...  2.37 us
  transfers between devices with their start and end apart: 8, of which 0 were waited for; matrix products, arithmetic and copies ran while one was open for 0% of the time, Pallas kernels for 37%

profile of v2, /device:TPU:21, one launch (start us, length us, event | category | flops | bytes accessed | tf_op | source)
XLA Modules:
  0.0 40.3 jit_solution(6779141506462087113)
XLA Ops:
  0.0 5.6 %edges.1 = (bf16[1536,1536]{1,0:T(8,128)(2,1)S(1)}, bf16[1536,1536]{1,0:T(8,128)(2,1)S(1)}, bf16[1536,512]{1,0:T(8,128)(2,1)S(1)}, f32[136,128]{1,0:T(8,128)S(1)...) custom-call(s32[12]{0:T(128)} %bitcast.11, bf16[1536,1536]{1,0:T(8,128)(2,1)} %bitcast.9, bf16[1536,1536]{1,0:T(8,128)(2,1)} %bitcast.10, ...), custom_call_target="tpu_custom_call" | custom-call | flops 3000000000 | bytes 8000000 | tf_op jit(solution)/shard_map/edges/pallas_call | solution.py:361
  5.6 1.1 %collective-permute-start = (f32[136,128]{1,0:T(8,128)S(1)}, f32[136,128]{1,0:T(8,128)S(1)}, u32[]{:S(2)}, u32[]{:S(2)}) collective-permute-start(f32[136,128]{1,0:T(8,128)S(1)} %get-tuple-element.28), channel_id=1, source_target_pairs={{0,8},{16,24},{8,0},{24,16},{1,9},{17,25},{9,1},{25,17},{2,10},{18... | collective-permute-start | bytes 208904 | tf_op jit(solution)/shard_map/ppermute | solution.py:321
  6.7 1.9 %collective-permute-start.1 = (f32[136,128]{1,0:T(8,128)S(1)}, f32[136,128]{1,0:T(8,128)S(1)}, u32[]{:S(2)}, u32[]{:S(2)}) collective-permute-start(f32[136,128]{1,0:T(8,128)S(1)} %get-tuple-element.29), channel_id=1, source_target_pairs={{8,16},{16,8},{9,17},{17,9},{10,18},{18,10},{11,19},{19,11},{12,20... | collective-permute-start | bytes 208904 | tf_op jit(solution)/shard_map/ppermute | solution.py:321
  8.6 4.1 %faces.1 = (bf16[1536,512]{1,0:T(8,128)(2,1)S(1)}, f32[1032,128]{1,0:T(8,128)S(1)}, f32[1032,128]{1,0:T(8,128)S(1)}) custom-call(s32[12]{0:T(128)} %bitcast.12, bf16[1536,1536]{1,0:T(8,128)(2,1)} %bitcast.6, bf16[1536,1536]{1,0:T(8,128)(2,1)S(1)} %get-tuple-element.22.lbuf, bf16[1536,1536]{1,0:T(8,128)(2,1)S(1)} %get-tuple-element.23.cbuf, ...), custom_call_target="tpu_custom_call" | custom-call | flops 3000000000 | bytes 1000000 | tf_op jit(solution)/shard_map/faces/pallas_call | solution.py:380
  12.7 0.0 collective-permute-done.fya
  12.7 0.0 collective-permute-done.1.fyb
  12.7 5.6 %collective-permute-start.3 = (f32[1032,128]{1,0:T(8,128)S(1)}, f32[1032,128]{1,0:T(8,128)S(1)}, u32[]{:S(2)}, u32[]{:S(2)}) collective-permute-start(f32[1032,128]{1,0:T(8,128)S(1)} %get-tuple-element.31.zb), channel_id=1, source_target_pairs={{1,2},{3,4},{5,6},{2,1},{4,3},{6,5},{9,10},{11,12},{13,14},{10,9},... | collective-permute-start | bytes 1585160 | tf_op jit(solution)/shard_map/ppermute | solution.py:321
  18.3 0.1 collective-permute-start.2
  18.4 4.8 %sides.1 = (bf16[1536,512]{1,0:T(8,128)(2,1)S(1)}, f32[512,128]{1,0:T(8,128)S(1)}, f32[512,128]{1,0:T(8,128)S(1)}, f32[128,128]{1,0:T(8,128)S(1)}, f32[128,128]{1,0:T(8,128)S(1)}, /*index=5*/f32[1024,128]{1,0:T(8,128)S(1)}) custom-call(s32[12]{0:T(128)} %bitcast.13, bf16[1536,1536]{1,0:T(8,128)(2,1)} %bitcast.7, ...), custom_call_target="tpu_custom_call" | custom-call | flops 3000000000 | bytes 1000000 | tf_op jit(solution)/shard_map/sides/pallas_call | solution.py:402
  23.3 1.5 %collective-permute-start.6 = (f32[128,128]{1,0:T(8,128)S(1)}, f32[128,128]{1,0:T(8,128)S(1)}, u32[]{:S(2)}, u32[]{:S(2)}) collective-permute-start(f32[128,128]{1,0:T(8,128)S(1)} %get-tuple-element.34.xa), channel_id=1, source_target_pairs={{0,32},{64,96},{32,0},{96,64},{1,33},{65,97},{33,1},{97,65},{2,34}... | collective-permute-start | bytes 196616 | tf_op jit(solution)/shard_map/ppermute | solution.py:321
  24.7 3.6 %collective-permute-start.7 = (f32[128,128]{1,0:T(8,128)S(1)}, f32[128,128]{1,0:T(8,128)S(1)}, u32[]{:S(2)}, u32[]{:S(2)}) collective-permute-start(f32[128,128]{1,0:T(8,128)S(1)} %get-tuple-element.35.xb), channel_id=1, source_target_pairs={{32,64},{64,32},{33,65},{65,33},{34,66},{66,34},{35,67},{67,35},{3... | collective-permute-start | bytes 196616 | tf_op jit(solution)/shard_map/ppermute | solution.py:321
  28.4 0.1 collective-permute-start.4
  28.5 0.0 collective-permute-done.6.fxa
  28.5 3.5 %collective-permute-start.5 = (f32[512,128]{1,0:T(8,128)S(1)}, f32[512,128]{1,0:T(8,128)S(1)}, u32[]{:S(2)}, u32[]{:S(2)}) collective-permute-start(f32[512,128]{1,0:T(8,128)S(1)} %get-tuple-element.33.yeb), channel_id=1, source_target_pairs={{8,16},{16,8},{9,17},{17,9},{10,18},{18,10},{11,19},{19,11},{12,20... | collective-permute-start | bytes 786440 | tf_op jit(solution)/shard_map/ppermute | solution.py:321
  32.0 5.9 %rest.1.before = f32[1536,1536]{1,0:T(8,128)} custom-call(s32[12]{0:T(128)} %bitcast.14, bf16[1536,1536]{1,0:T(8,128)(2,1)} %bitcast.8, bf16[1536,512]{1,0:T(8,128)(2,1)S(1)} %get-tuple-element.24.wbd, bf16[1536,512]{1,0:T(8,128)(2,1)S(1)} %get-tuple-element.36.wac, bf16[1536,512]{1,0:T(8,128)(2,1)S(1)} %get-tuple-element.37.wef, ...), custom_call_target="tpu_custom_call" | custom-call | flops 3000000000 | bytes 8000000 | tf_op jit(solution)/shard_map/rest/pallas_call | solution.py:423
  37.9 0.0 collective-permute-done.7.fxb
  37.9 0.0 collective-permute-done.4.fyea
  37.9 0.0 collective-permute-done.5.fyeb
  37.9 0.0 collective-permute-done.3.fzb
  38.0 0.0 collective-permute-done.2.fza
  38.0 2.4 %last.1 = f32[1536,1536]{1,0:T(8,128)} custom-call(s32[12]{0:T(128)} %bitcast.15, f32[1032,128]{1,0:T(8,128)S(1)} %get-tuple-element.30.after.za, f32[1032,128]{1,0:T(8,128)S(1)} %get-tuple-element.31.zb, f32[1032,128]{1,0:T(8,128)S(1)} %collective-permute-done.2.fza, f32[1032,128]{1,0:T(8,128)S(1)} %collective-permute-done.3.fzb, ...), custom_call_target="tpu_custom_call", output_to_operand_aliasing={{}: (13, {})} | custom-call | flops 100000000 | bytes 3000000 | tf_op jit(solution)/shard_map/last/pallas_call | solution.py:441
  (1 shorter events, 0.0 us)
Async XLA Ops:
  5.6 7.1 %collective-permute-start = (f32[136,128]{1,0:T(8,128)S(1)}, f32[136,128]{1,0:T(8,128)S(1)}, u32[]{:S(2)}, u32[]{:S(2)}) collective-permute-start(f32[136,128]{1,0:T(8,128)S(1)} %get-tuple-element.28), channel_id=1, source_target_pairs={{0,8},{16,24},{8,0},{24,16},{1,9},{17,25},{9,1},{25,17},{2,10},{18... | collective-permute-start | bytes 208904 | tf_op jit(solution)/shard_map/ppermute | solution.py:321
  6.7 6.0 %collective-permute-start.1 = (f32[136,128]{1,0:T(8,128)S(1)}, f32[136,128]{1,0:T(8,128)S(1)}, u32[]{:S(2)}, u32[]{:S(2)}) collective-permute-start(f32[136,128]{1,0:T(8,128)S(1)} %get-tuple-element.29), channel_id=1, source_target_pairs={{8,16},{16,8},{9,17},{17,9},{10,18},{18,10},{11,19},{19,11},{12,20... | collective-permute-start | bytes 208904 | tf_op jit(solution)/shard_map/ppermute | solution.py:321
  12.7 25.2 %collective-permute-start.3 = (f32[1032,128]{1,0:T(8,128)S(1)}, f32[1032,128]{1,0:T(8,128)S(1)}, u32[]{:S(2)}, u32[]{:S(2)}) collective-permute-start(f32[1032,128]{1,0:T(8,128)S(1)} %get-tuple-element.31.zb), channel_id=1, source_target_pairs={{1,2},{3,4},{5,6},{2,1},{4,3},{6,5},{9,10},{11,12},{13,14},{10,9},... | collective-permute-start | bytes 1585160 | tf_op jit(solution)/shard_map/ppermute | solution.py:321
  18.3 19.6 %collective-permute-start.2 = (f32[1032,128]{1,0:T(8,128)S(1)}, f32[1032,128]{1,0:T(8,128)S(1)}, u32[]{:S(2)}, u32[]{:S(2)}) collective-permute-start(f32[1032,128]{1,0:T(8,128)S(1)} %get-tuple-element.30.after.za), channel_id=1, source_target_pairs={{0,1},{2,3},{4,5},{6,7},{1,0},{3,2},{5,4},{7,6},{8,9},{10,11},{12,... | collective-permute-start | bytes 1585160 | tf_op jit(solution)/shard_map/ppermute | solution.py:321
  23.3 5.2 %collective-permute-start.6 = (f32[128,128]{1,0:T(8,128)S(1)}, f32[128,128]{1,0:T(8,128)S(1)}, u32[]{:S(2)}, u32[]{:S(2)}) collective-permute-start(f32[128,128]{1,0:T(8,128)S(1)} %get-tuple-element.34.xa), channel_id=1, source_target_pairs={{0,32},{64,96},{32,0},{96,64},{1,33},{65,97},{33,1},{97,65},{2,34}... | collective-permute-start | bytes 196616 | tf_op jit(solution)/shard_map/ppermute | solution.py:321
  24.7 13.2 %collective-permute-start.7 = (f32[128,128]{1,0:T(8,128)S(1)}, f32[128,128]{1,0:T(8,128)S(1)}, u32[]{:S(2)}, u32[]{:S(2)}) collective-permute-start(f32[128,128]{1,0:T(8,128)S(1)} %get-tuple-element.35.xb), channel_id=1, source_target_pairs={{32,64},{64,32},{33,65},{65,33},{34,66},{66,34},{35,67},{67,35},{3... | collective-permute-start | bytes 196616 | tf_op jit(solution)/shard_map/ppermute | solution.py:321
  28.4 9.6 %collective-permute-start.4 = (f32[512,128]{1,0:T(8,128)S(1)}, f32[512,128]{1,0:T(8,128)S(1)}, u32[]{:S(2)}, u32[]{:S(2)}) collective-permute-start(f32[512,128]{1,0:T(8,128)S(1)} %get-tuple-element.32.yea), channel_id=1, source_target_pairs={{0,8},{16,24},{8,0},{24,16},{1,9},{17,25},{9,1},{25,17},{2,10},{18... | collective-permute-start | bytes 786440 | tf_op jit(solution)/shard_map/ppermute | solution.py:321
  28.5 9.5 %collective-permute-start.5 = (f32[512,128]{1,0:T(8,128)S(1)}, f32[512,128]{1,0:T(8,128)S(1)}, u32[]{:S(2)}, u32[]{:S(2)}) collective-permute-start(f32[512,128]{1,0:T(8,128)S(1)} %get-tuple-element.33.yeb), channel_id=1, source_target_pairs={{8,16},{16,8},{9,17},{17,9},{10,18},{18,10},{11,19},{19,11},{12,20... | collective-permute-start | bytes 786440 | tf_op jit(solution)/shard_map/ppermute | solution.py:321

commit v3 on v2

--- a/solution.py
+++ b/solution.py
@@ -42,15 +42,12 @@
 
 
 def stiff_copies(at, stiff, buf, sem, blocks):
-    copies = [
+    return [
         pltpu.make_async_copy(
             stiff.at[pl.ds(at[k], BLK), pl.ds(at[l], BLK)], buf.at[pl.ds(n * BLK, BLK), :], sem
         )
         for n, (k, l) in enumerate(blocks)
     ]
-    for copy in copies:
-        copy.start()
-    return copies
 
 
 def weigh(lbuf, cbuf, columns, pan):
@@ -95,10 +92,21 @@
     return slice(n * BLK, (n + 1) * BLK)
 
 
+FACE_BLOCKS = ((4, 4), (4, 5), (5, 5), (4, 8), (4, 9), (5, 8), (5, 9), (6, 6), (6, 7), (7, 7), (6, 10), (6, 11), (7, 10), (7, 11))
+SIDE_BLOCKS = tuple((k, l) for k in (2, 3) for l in (2, 3, 8, 9, 10, 11) if k <= l) + ((8, 10), (8, 11), (9, 10), (9, 11), (0, 0), (0, 1), (1, 1))
+REST = (
+    ("F", (("bd", (8, 9, 10, 11)), ("ac", (4, 5, 6, 7)), ("e", (2, 3)))),
+    ("E", (("ac", (4, 5, 6, 7)),)),
+    ("A", (("c", (6, 7)), ("d", (10, 11)))),
+    ("C", (("b", (8, 9)),)),
+)
+REST_BLOCKS = tuple((k, l) for left, rights in REST for _, cols in rights for k in PAIRS[left] for l in cols)
+LATER = FACE_BLOCKS + SIDE_BLOCKS + REST_BLOCKS
+AT_FACES, AT_SIDES, AT_REST = 0, len(FACE_BLOCKS), len(FACE_BLOCKS) + len(SIDE_BLOCKS)
 EDGE_BLOCKS = ((8, 8), (8, 9), (9, 9), (10, 10), (10, 11), (11, 11))
 
 
-def edge_kernel(order, inverse, coupling, stiff, lbuf, cbuf, wbd, yda, ydb, zpart, osmem, sbuf, osem, lsem, csem, rsem, ssem):
+def edge_kernel(order, inverse, coupling, stiff, lbuf, cbuf, sall, wbd, yda, ydb, zpart, osmem, sbuf, osem, lsem, csem, rsem, ssem):
     fetch = fetch_order(order, osmem, osem)
     panels = lbuf.shape[0] // PAN
     lcopies = [
@@ -128,18 +136,22 @@
         for copy in group:
             copy.start()
     scopies = stiff_copies(at, stiff, sbuf, ssem, EDGE_BLOCKS)
+    for copy in scopies:
+        copy.start()
     later = [
         pltpu.make_async_copy(
             coupling.at[:, pl.ds(at[k], BLK)], cbuf.at[:, pl.ds((n + 4) * BLK, BLK)], rsem
         )
         for n, k in enumerate(COLUMNS[4:])
     ]
-    for copy in later:
-        copy.start()
+    later += stiff_copies(at, stiff, sall, rsem, LATER)
     for pan in range(panels):
         lcopies[pan].wait()
         for copy in ccopies[pan]:
             copy.wait()
+        if pan == 2:
+            for copy in later:
+                copy.start()
         wbd[pan * PAN : (pan + 1) * PAN, :] = weigh(lbuf, cbuf, slice(0, 512), pan)
     for copy in scopies:
         copy.wait()
@@ -163,25 +175,17 @@
         copy.wait()
 
 
-FACE_BLOCKS = ((4, 4), (4, 5), (5, 5), (4, 8), (4, 9), (5, 8), (5, 9), (6, 6), (6, 7), (7, 7), (6, 10), (6, 11), (7, 10), (7, 11))
-
-
-def face_kernel(order, stiff, lbuf, cbuf, wbd, zpart, wac, za, zb, osmem, sbuf, osem, ssem):
-    fetch_order(order, osmem, osem).wait()
-    at = positions(osmem)
-    scopies = stiff_copies(at, stiff, sbuf, ssem, FACE_BLOCKS)
+def face_kernel(sall, lbuf, cbuf, wbd, zpart, wac, za, zb):
     for pan in range(lbuf.shape[0] // PAN):
         wac[pan * PAN : (pan + 1) * PAN, :] = weigh(lbuf, cbuf, slice(512, 1024), pan)
-    for copy in scopies:
-        copy.wait()
     for n, (out, part) in enumerate(((zb, 0), (za, 1))):
         own = wac[:, n * 256 : (n + 1) * 256]
         inner = gram(own, own)
         outer = gram(own, wbd[:, n * 256 : (n + 1) * 256])
-        base = n * 7
+        base = AT_FACES + n * 7
 
         def value(m, result, i, j):
-            return sbuf[slot(base + m)].astype(jnp.float32) - piece(result, i, j)
+            return sall[slot(base + m)].astype(jnp.float32) - piece(result, i, j)
 
         out[slot(6)], row = pack(value(0, inner, 0, 0), value(2, inner, 1, 1))
         out[slot(0)] = value(1, inner, 0, 1)
@@ -203,18 +207,10 @@
     zb_out[FACES:] = zb_out[FACES:] + jnp.where(row, fya[BLK : BLK + 1], 0.0)
 
 
-SIDE_BLOCKS = tuple((k, l) for k in (2, 3) for l in (2, 3, 8, 9, 10, 11) if k <= l) + ((8, 10), (8, 11), (9, 10), (9, 11), (0, 0), (0, 1), (1, 1))
-
-
-def side_kernel(order, stiff, lbuf, cbuf, wbd, after, wef, yea, yeb, xa, xb, keep, osmem, sbuf, osem, ssem):
+def side_kernel(sall, lbuf, cbuf, wbd, after, wef, yea, yeb, xa, xb, keep):
     del after
-    fetch_order(order, osmem, osem).wait()
-    at = positions(osmem)
-    scopies = stiff_copies(at, stiff, sbuf, ssem, SIDE_BLOCKS)
     for pan in range(lbuf.shape[0] // PAN):
         wef[pan * PAN : (pan + 1) * PAN, :] = weigh(lbuf, cbuf, slice(1024, 1536), pan)
-    for copy in scopies:
-        copy.wait()
     e, f = wef[:, :256], wef[:, 256:]
     targets = {pair: (yea, n) for n, pair in enumerate(Y_HIGH)} | {pair: (yeb, n) for n, pair in enumerate(Y_LOW)}
     targets |= {pair: (keep, n) for n, pair in enumerate(KEPT)} | {(1, 1): (xa, 0), (0, 0): (xb, 0)}
@@ -224,8 +220,8 @@
             for j, l in enumerate(cols):
                 if k <= l:
                     out, n = targets[(k, l)]
-                    m = SIDE_BLOCKS.index((k, l))
-                    out[slot(n)] = sbuf[slot(m)].astype(jnp.float32) - piece(result, i, j)
+                    m = AT_SIDES + SIDE_BLOCKS.index((k, l))
+                    out[slot(n)] = sall[slot(m)].astype(jnp.float32) - piece(result, i, j)
 
     emit(gram(e, e), (2, 3), (2, 3))
     emit(gram(e, wbd[...]), (2, 3), (8, 9, 10, 11))
@@ -233,86 +229,83 @@
     emit(gram(f, f), (0, 1), (0, 1))
 
 
-REST = (
-    ("F", (("bd", (8, 9, 10, 11)), ("ac", (4, 5, 6, 7)), ("e", (2, 3)))),
-    ("E", (("ac", (4, 5, 6, 7)),)),
-    ("A", (("c", (6, 7)), ("d", (10, 11)))),
-    ("C", (("b", (8, 9)),)),
-)
-REST_BLOCKS = tuple((k, l) for left, rights in REST for _, cols in rights for k in PAIRS[left] for l in cols)
-
-
-def put(at, out, stage, sem, n, k, l):
-    copy = pltpu.make_async_copy(
-        stage.at[pl.ds(n * BLK, BLK), :], out.at[pl.ds(at[k], BLK), pl.ds(at[l], BLK)], sem
-    )
-    copy.start()
-    return copy
-
-
-def rest_kernel(order, stiff, wbd, wac, wef, keep, out, osmem, sbuf, turned, stage, osem, ssem, wsem):
-    fetch_order(order, osmem, osem).wait()
-    at = positions(osmem)
-    scopies = stiff_copies(at, stiff, sbuf, ssem, REST_BLOCKS)
-    copies = []
-
-    def emit(k, l, value):
-        n = len(copies)
-        stage[slot(n)] = value
-        copies.append(put(at, out, stage, wsem, n, k, l))
-        stage[slot(n + 1)] = value.T
-        copies.append(put(at, out, stage, wsem, n + 1, l, k))
-
+class Writer:
+    def __init__(self, order, osmem, osem, out, stage, sem):
+        self.fetch = fetch_order(order, osmem, osem)
+        self.osmem, self.out, self.stage, self.sem = osmem, out, stage, sem
+        self.cells, self.copies, self.at = [], [], None
+
+    def ready(self):
+        self.fetch.wait()
+        self.at = positions(self.osmem)
+        self.flush()
+
+    def flush(self):
+        if self.at is not None:
+            for n in range(len(self.copies), len(self.cells)):
+                k, l = self.cells[n]
+                copy = pltpu.make_async_copy(
+                    self.stage.at[pl.ds(n * BLK, BLK), :],
+                    self.out.at[pl.ds(self.at[k], BLK), pl.ds(self.at[l], BLK)],
+                    self.sem,
+                )
+                copy.start()
+                self.copies.append(copy)
+
+    def emit(self, k, l, value):
+        self.stage[slot(len(self.cells))] = value
+        self.cells.append((k, l))
+        if k != l:
+            self.stage[slot(len(self.cells))] = value.T
+            self.cells.append((l, k))
+        self.flush()
+
+    def finish(self):
+        for copy in self.copies:
+            copy.wait()
+
+
+def rest_kernel(order, sall, wbd, wac, wef, keep, out, osmem, turned, stage, osem, wsem):
+    writer = Writer(order, osmem, osem, out, stage, wsem)
     whole = {"ac": (wac, 0, 512), "bd": (wbd, 0, 512), "e": (wef, 0, 256), "f": (wef, 256, 512), "a": (wac, 0, 256)}
     whole |= {"c": (wac, 256, 512), "b": (wbd, 0, 256), "d": (wbd, 256, 512)}
     for n, (k, l) in enumerate(KEPT):
-        emit(k, l, keep[slot(n)])
-    for copy in scopies:
-        copy.wait()
-    m = 0
+        writer.emit(k, l, keep[slot(n)])
+    m = AT_REST
     for left, rights in REST:
         ref, lo, hi = whole[left.lower()]
         turned[...] = ref[:, lo:hi].T
         for name, cols in rights:
             ref, lo, hi = whole[name]
             result = jnp.dot(turned[...], ref[:, lo:hi], preferred_element_type=jnp.float32)
+            if writer.at is None:
+                writer.ready()
             for i, k in enumerate(PAIRS[left]):
                 for j, l in enumerate(cols):
-                    emit(k, l, sbuf[slot(m)].astype(jnp.float32) - piece(result, i, j))
+                    writer.emit(k, l, sall[slot(m)].astype(jnp.float32) - piece(result, i, j))
                     m += 1
-    for copy in copies:
-        copy.wait()
+    writer.finish()
 
 
 def last_kernel(order, za, zb, fza, fzb, yea, yeb, fyea, fyeb, xa, xb, fxa, fxb, before, out, osmem, stage, osem, wsem):
     del before
-    fetch_order(order, osmem, osem).wait()
-    at = positions(osmem)
-    copies = []
-
-    def emit(k, l, value):
-        n = len(copies)
-        stage[slot(n)] = value
-        copies.append(put(at, out, stage, wsem, n, k, l))
-        if k != l:
-            stage[slot(n + 1)] = value.T
-            copies.append(put(at, out, stage, wsem, n + 1, l, k))
-
-    emit(0, 0, xb[...] + fxb[...])
-    emit(1, 1, xa[...] + fxa[...])
-    for pairs, own, other in ((Y_HIGH, yea, fyea), (Y_LOW, yeb, fyeb)):
-        for n, (k, l) in enumerate(pairs):
-            emit(k, l, own[slot(n)] + other[slot(n)])
+    writer = Writer(order, osmem, osem, out, stage, wsem)
     for pairs, packs, own, other in ((Z_LOW, Z_LOW_PACK, zb, fzb), (Z_HIGH, Z_HIGH_PACK, za, fza)):
         for n, (k, l) in enumerate(pairs):
-            emit(k, l, own[slot(n)] + other[slot(n)])
+            writer.emit(k, l, own[slot(n)] + other[slot(n)])
         for n, (k, l) in enumerate(packs):
             row = slice(FACES + n, FACES + n + 1)
             first, second = unpack(own[slot(6 + n)] + other[slot(6 + n)], own[row] + other[row])
-            emit(k, k, first)
-            emit(l, l, second)
-    for copy in copies:
-        copy.wait()
+            writer.emit(k, k, first)
+            writer.emit(l, l, second)
+        if writer.at is None:
+            writer.ready()
+    for pairs, own, other in ((Y_HIGH, yea, fyea), (Y_LOW, yeb, fyeb)):
+        for n, (k, l) in enumerate(pairs):
+            writer.emit(k, l, own[slot(n)] + other[slot(n)])
+    writer.emit(0, 0, xb[...] + fxb[...])
+    writer.emit(1, 1, xa[...] + fxa[...])
+    writer.finish()
 
 
 def exchange(value, axis, start):
@@ -355,22 +348,20 @@
     panels = rows // PAN
     osmem = pltpu.SMEM((NBLK,), jnp.int32)
 
-    def stiff_scratch(blocks):
-        return pltpu.VMEM((len(blocks) * BLK, BLK), half)
-
-    lbuf, cbuf, wbd, yda, ydb, zpart = pl.pallas_call(
+    lbuf, cbuf, sall, wbd, yda, ydb, zpart = pl.pallas_call(
         edge_kernel,
         out_shape=(
             shape(rows, rows, dtype=half),
             shape(rows, size, dtype=half),
+            shape(len(LATER) * BLK, BLK, dtype=half),
             shape(rows, 512, dtype=half),
             shape(BLK + 8, BLK),
             shape(BLK + 8, BLK),
             shape(4 * BLK + 8, BLK),
         ),
         in_specs=[HBM] * 4,
-        out_specs=(VMEM,) * 6,
-        scratch_shapes=[osmem, stiff_scratch(EDGE_BLOCKS), DMA, DMA((panels,)), DMA((panels,)), DMA, DMA],
+        out_specs=(VMEM,) * 7,
+        scratch_shapes=[osmem, pltpu.VMEM((len(EDGE_BLOCKS) * BLK, BLK), half), DMA, DMA((panels,)), DMA((panels,)), DMA, DMA],
         compiler_params=params(12),
         cost_estimate=cost(3, 8),
         name="edges",
@@ -380,13 +371,12 @@
     wac, za, zb = pl.pallas_call(
         face_kernel,
         out_shape=(shape(rows, 512, dtype=half), shape(MESSAGE, BLK), shape(MESSAGE, BLK)),
-        in_specs=[HBM, HBM] + [VMEM] * 4,
+        in_specs=[VMEM] * 5,
         out_specs=(VMEM,) * 3,
-        scratch_shapes=[osmem, stiff_scratch(FACE_BLOCKS), DMA, DMA],
         compiler_params=params(12),
         cost_estimate=cost(3, 1),
         name="faces",
-    )(order, stiff, lbuf, cbuf, wbd, zpart)
+    )(sall, lbuf, cbuf, wbd, zpart)
     za, zb = pl.pallas_call(
         join_kernel,
         out_shape=(shape(MESSAGE, BLK), shape(MESSAGE, BLK)),
@@ -409,13 +399,12 @@
             shape(BLK, BLK),
             shape(len(KEPT) * BLK, BLK),
         ),
-        in_specs=[HBM, HBM] + [VMEM] * 4,
+        in_specs=[VMEM] * 5,
         out_specs=(VMEM,) * 6,
-        scratch_shapes=[osmem, stiff_scratch(SIDE_BLOCKS), DMA, DMA],
         compiler_params=params(12),
         cost_estimate=cost(3, 1),
         name="sides",
-    )(order, stiff, lbuf, cbuf, wbd, za)
+    )(sall, lbuf, cbuf, wbd, za)
     fyea = exchange(yea, "gy", 0)
     fyeb = exchange(yeb, "gy", 1)
     fxa = exchange(xa, "gx", 0)
@@ -423,21 +412,19 @@
     out = pl.pallas_call(
         rest_kernel,
         out_shape=shape(size, size),
-        in_specs=[HBM, HBM] + [VMEM] * 4,
+        in_specs=[HBM] + [VMEM] * 5,
         out_specs=HBM,
         scratch_shapes=[
             osmem,
-            stiff_scratch(REST_BLOCKS),
             pltpu.VMEM((PAN, rows), half),
             pltpu.VMEM((2 * (len(KEPT) + len(REST_BLOCKS)) * BLK, BLK), jnp.float32),
-            DMA,
             DMA,
             DMA,
         ],
         compiler_params=params(16),
         cost_estimate=cost(3, 8),
         name="rest",
-    )(order, stiff, wbd, wac, wef, keep)
+    )(order, sall, wbd, wac, wef, keep)
     out = pl.pallas_call(
         last_kernel,
         out_shape=shape(size, size),

time: 41 us -> 36.5 us (0.89)
  Pallas kernels: 22.8 us -> 16.7 us
  waiting for transfers between devices: 0.02 us -> 2.64 us
  starting transfers between devices: 17.3 us -> 16.8 us
    ppermute x8, waiting for transfers between devices: 0.02 us -> 2.64 us  [exchange(): return lax.ppermute(value, axis, pairs + [(j, i) for i, j in pairs])]
    pallas_call x1, Pallas kernels: 4.83 us -> 2.66 us  [shards(): pl.pallas_call(side_kernel, out_shape=(shape(rows, 512, dtype=half), shap...]
    pallas_call x1, Pallas kernels: 5.95 us -> 4.07 us  [shards(): pl.pallas_call(rest_kernel, out_shape=shape(size, size), in_specs=[HBM] +...]
    pallas_call x1, Pallas kernels: 4.08 us -> 2.45 us  [shards(): pl.pallas_call(face_kernel, out_shape=(shape(rows, 512, dtype=half), shap...]
    ppermute x8, starting transfers between devices: 17.3 us -> 16.8 us  [exchange(): return lax.ppermute(value, axis, pairs + [(j, i) for i, j in pairs])]
    pallas_call x1, Pallas kernels: 5.59 us -> 5.14 us  [shards(): pl.pallas_call(edge_kernel, out_shape=(shape(rows, rows, dtype=half), sha...]
  transfers between devices with their start and end apart: 8 -> 8, of which waited for: 0 -> 3; matrix products, arithmetic and copies ran while one was open for 0% -> 0% of each run, Pallas kernels for 37% -> 25%
where the time goes in v3:
time: 36.5 us; the launch traced here: 36.2 us
  starting transfers between devices  16.8 us (46%)
  Pallas kernels  16.7 us (46%)
  waiting for transfers between devices  2.64 us (7%)
    ppermute x8, starting transfers between devices, exchange(): return lax.ppermute(value, axis, pairs + [(j, i) for i, j in pairs])  16.8 us
    pallas_call x1, Pallas kernels, shards(): pl.pallas_call(edge_kernel, out_shape=(shape(rows, rows, dtype=half), sha...  5.14 us
    pallas_call x1, Pallas kernels, shards(): pl.pallas_call(rest_kernel, out_shape=shape(size, size), in_specs=[HBM] +...  4.07 us
    pallas_call x1, Pallas kernels, shards(): pl.pallas_call(side_kernel, out_shape=(shape(rows, 512, dtype=half), shap...  2.66 us
    ppermute x8, waiting for transfers between devices, exchange(): return lax.ppermute(value, axis, pairs + [(j, i) for i, j in pairs])  2.64 us
    pallas_call x1, Pallas kernels, shards(): pl.pallas_call(face_kernel, out_shape=(shape(rows, 512, dtype=half), shap...  2.45 us
    pallas_call x1, Pallas kernels, shards(): pl.pallas_call(last_kernel, out_shape=shape(size, size), in_specs=[HBM] +...  2.32 us
  transfers between devices with their start and end apart: 8, of which 3 were waited for; matrix products, arithmetic and copies ran while one was open for 0% of the time, Pallas kernels for 25%

profile of v3, /device:TPU:21, one launch (start us, length us, event | category | flops | bytes accessed | tf_op | source)
XLA Modules:
  0.0 36.2 jit_solution(5370137458829807153)
XLA Ops:
  0.0 5.1 %edges.1 = (bf16[1536,1536]{1,0:T(8,128)(2,1)S(1)}, bf16[1536,1536]{1,0:T(8,128)(2,1)S(1)}, bf16[9216,128]{1,0:T(8,128)(2,1)S(1)}, bf16[1536,512]{1,0:T(8,128)(2...) custom-call(s32[12]{0:T(128)} %bitcast.8, bf16[1536,1536]{1,0:T(8,128)(2,1)} %bitcast.5, ...), custom_call_target="tpu_custom_call" | custom-call | flops 3000000000 | bytes 8000000 | tf_op jit(solution)/shard_map/edges/pallas_call | solution.py:351
  5.1 1.1 %collective-permute-start = (f32[136,128]{1,0:T(8,128)S(1)}, f32[136,128]{1,0:T(8,128)S(1)}, u32[]{:S(2)}, u32[]{:S(2)}) collective-permute-start(f32[136,128]{1,0:T(8,128)S(1)} %get-tuple-element.30), channel_id=1, source_target_pairs={{0,8},{16,24},{8,0},{24,16},{1,9},{17,25},{9,1},{25,17},{2,10},{18... | collective-permute-start | bytes 208904 | tf_op jit(solution)/shard_map/ppermute | solution.py:314
  6.2 1.9 %collective-permute-start.1 = (f32[136,128]{1,0:T(8,128)S(1)}, f32[136,128]{1,0:T(8,128)S(1)}, u32[]{:S(2)}, u32[]{:S(2)}) collective-permute-start(f32[136,128]{1,0:T(8,128)S(1)} %get-tuple-element.31), channel_id=1, source_target_pairs={{8,16},{16,8},{9,17},{17,9},{10,18},{18,10},{11,19},{19,11},{12,20... | collective-permute-start | bytes 208904 | tf_op jit(solution)/shard_map/ppermute | solution.py:314
  8.1 2.4 %faces.1 = (bf16[1536,512]{1,0:T(8,128)(2,1)S(1)}, f32[1032,128]{1,0:T(8,128)S(1)}, f32[1032,128]{1,0:T(8,128)S(1)}) custom-call(bf16[9216,128]{1,0:T(8,128)(2,1)S(1)} %get-tuple-element.23.sall, bf16[1536,1536]{1,0:T(8,128)(2,1)S(1)} %get-tuple-element.24.lbuf, bf16[1536,1536]{1,0:T(8,128)(2,1)S(1)} %get-tuple-element.25.cbuf, ...), custom_call_target="tpu_custom_call" | custom-call | flops 3000000000 | bytes 1000000 | tf_op jit(solution)/shard_map/faces/pallas_call | solution.py:371
  10.6 0.0 collective-permute-done.fya
  10.6 0.7 %collective-permute-done.1.fyb = f32[136,128]{1,0:T(8,128)S(1)} collective-permute-done((f32[136,128]{1,0:T(8,128)S(1)}, f32[136,128]{1,0:T(8,128)S(1)}, u32[]{:S(2)}, u32[]{:S(2)}) %collective-permute-start.1) | collective-permute-done | bytes 69664 | tf_op jit(solution)/shard_map/ppermute | solution.py:314
  11.3 5.6 %collective-permute-start.3 = (f32[1032,128]{1,0:T(8,128)S(1)}, f32[1032,128]{1,0:T(8,128)S(1)}, u32[]{:S(2)}, u32[]{:S(2)}) collective-permute-start(f32[1032,128]{1,0:T(8,128)S(1)} %get-tuple-element.33.zb), channel_id=1, source_target_pairs={{1,2},{3,4},{5,6},{2,1},{4,3},{6,5},{9,10},{11,12},{13,14},{10,9},... | collective-permute-start | bytes 1585160 | tf_op jit(solution)/shard_map/ppermute | solution.py:314
  16.9 0.1 collective-permute-start.2
  17.0 2.7 %sides.1 = (bf16[1536,512]{1,0:T(8,128)(2,1)S(1)}, f32[512,128]{1,0:T(8,128)S(1)}, f32[512,128]{1,0:T(8,128)S(1)}, f32[128,128]{1,0:T(8,128)S(1)}, f32[128,128]{1,0:T(8,128)S(1)}, /*index=5*/f32[1024,128]{1,0:T(8,128)S(1)}) custom-call(bf16[9216,128]{1,0:T(8,128)(2,1)S(1)} %get-tuple-element.23.sall, bf16[1536,1536]{1,0:T(8,128)(2,1)S(1)} %get-tuple-element.24.lbuf, ...), custom_call_target="tpu_custom_call" | custom-call | flops 3000000000 | bytes 1000000 | tf_op jit(solution)/shard_map/sides/pallas_call | solution.py:392
  19.7 2.5 %collective-permute-start.6 = (f32[128,128]{1,0:T(8,128)S(1)}, f32[128,128]{1,0:T(8,128)S(1)}, u32[]{:S(2)}, u32[]{:S(2)}) collective-permute-start(f32[128,128]{1,0:T(8,128)S(1)} %get-tuple-element.36.xa), channel_id=1, source_target_pairs={{0,32},{64,96},{32,0},{96,64},{1,33},{65,97},{33,1},{97,65},{2,34}... | collective-permute-start | bytes 196616 | tf_op jit(solution)/shard_map/ppermute | solution.py:314
  22.2 3.5 %collective-permute-start.7 = (f32[128,128]{1,0:T(8,128)S(1)}, f32[128,128]{1,0:T(8,128)S(1)}, u32[]{:S(2)}, u32[]{:S(2)}) collective-permute-start(f32[128,128]{1,0:T(8,128)S(1)} %get-tuple-element.37.xb), channel_id=1, source_target_pairs={{32,64},{64,32},{33,65},{65,33},{34,66},{66,34},{35,67},{67,35},{3... | collective-permute-start | bytes 196616 | tf_op jit(solution)/shard_map/ppermute | solution.py:314
  25.8 0.1 collective-permute-start.4
  25.9 0.0 collective-permute-done.6.fxa
  25.9 1.9 %collective-permute-start.5 = (f32[512,128]{1,0:T(8,128)S(1)}, f32[512,128]{1,0:T(8,128)S(1)}, u32[]{:S(2)}, u32[]{:S(2)}) collective-permute-start(f32[512,128]{1,0:T(8,128)S(1)} %get-tuple-element.35.yeb), channel_id=1, source_target_pairs={{8,16},{16,8},{9,17},{17,9},{10,18},{18,10},{11,19},{19,11},{12,20... | collective-permute-start | bytes 786440 | tf_op jit(solution)/shard_map/ppermute | solution.py:314
  27.8 4.1 %rest.1.before = f32[1536,1536]{1,0:T(8,128)} custom-call(s32[12]{0:T(128)} %bitcast.9, bf16[9216,128]{1,0:T(8,128)(2,1)S(1)} %get-tuple-element.23.sall, bf16[1536,512]{1,0:T(8,128)(2,1)S(1)} %get-tuple-element.26.wbd, bf16[1536,512]{1,0:T(8,128)(2,1)S(1)} %get-tuple-element.38.wac, bf16[1536,512]{1,0:T(8,128)(2,1)S(1)} %get-tuple-element.39.wef, ...), custom_call_target="tpu_custom_call" | custom-call | flops 3000000000 | bytes 8000000 | tf_op jit(solution)/shard_map/rest/pallas_call | solution.py:412
  31.9 0.1 collective-permute-done.7.fxb
  32.0 0.0 collective-permute-done.4.fyea
  32.0 1.9 %collective-permute-done.5.fyeb = f32[512,128]{1,0:T(8,128)S(1)} collective-permute-done((f32[512,128]{1,0:T(8,128)S(1)}, f32[512,128]{1,0:T(8,128)S(1)}, u32[]{:S(2)}, u32[]{:S(2)}) %collective-permute-start.5) | collective-permute-done | bytes 262176 | tf_op jit(solution)/shard_map/ppermute | solution.py:314
  33.8 0.0 collective-permute-done.3.fzb
  33.8 0.0 collective-permute-done.2.fza
  33.8 2.3 %last.1 = f32[1536,1536]{1,0:T(8,128)} custom-call(s32[12]{0:T(128)} %bitcast.10, f32[1032,128]{1,0:T(8,128)S(1)} %get-tuple-element.32.after.za, f32[1032,128]{1,0:T(8,128)S(1)} %get-tuple-element.33.zb, f32[1032,128]{1,0:T(8,128)S(1)} %collective-permute-done.2.fza, f32[1032,128]{1,0:T(8,128)S(1)} %collective-permute-done.3.fzb, ...), custom_call_target="tpu_custom_call", output_to_operand_aliasing={{}: (13, {})} | custom-call | flops 100000000 | bytes 3000000 | tf_op jit(solution)/shard_map/last/pallas_call | solution.py:428
  (1 shorter events, 0.0 us)
Async XLA Ops:
  5.1 5.5 %collective-permute-start = (f32[136,128]{1,0:T(8,128)S(1)}, f32[136,128]{1,0:T(8,128)S(1)}, u32[]{:S(2)}, u32[]{:S(2)}) collective-permute-start(f32[136,128]{1,0:T(8,128)S(1)} %get-tuple-element.30), channel_id=1, source_target_pairs={{0,8},{16,24},{8,0},{24,16},{1,9},{17,25},{9,1},{25,17},{2,10},{18... | collective-permute-start | bytes 208904 | tf_op jit(solution)/shard_map/ppermute | solution.py:314
  6.2 5.0 %collective-permute-start.1 = (f32[136,128]{1,0:T(8,128)S(1)}, f32[136,128]{1,0:T(8,128)S(1)}, u32[]{:S(2)}, u32[]{:S(2)}) collective-permute-start(f32[136,128]{1,0:T(8,128)S(1)} %get-tuple-element.31), channel_id=1, source_target_pairs={{8,16},{16,8},{9,17},{17,9},{10,18},{18,10},{11,19},{19,11},{12,20... | collective-permute-start | bytes 208904 | tf_op jit(solution)/shard_map/ppermute | solution.py:314
  11.3 22.6 %collective-permute-start.3 = (f32[1032,128]{1,0:T(8,128)S(1)}, f32[1032,128]{1,0:T(8,128)S(1)}, u32[]{:S(2)}, u32[]{:S(2)}) collective-permute-start(f32[1032,128]{1,0:T(8,128)S(1)} %get-tuple-element.33.zb), channel_id=1, source_target_pairs={{1,2},{3,4},{5,6},{2,1},{4,3},{6,5},{9,10},{11,12},{13,14},{10,9},... | collective-permute-start | bytes 1585160 | tf_op jit(solution)/shard_map/ppermute | solution.py:314
  16.9 16.9 %collective-permute-start.2 = (f32[1032,128]{1,0:T(8,128)S(1)}, f32[1032,128]{1,0:T(8,128)S(1)}, u32[]{:S(2)}, u32[]{:S(2)}) collective-permute-start(f32[1032,128]{1,0:T(8,128)S(1)} %get-tuple-element.32.after.za), channel_id=1, source_target_pairs={{0,1},{2,3},{4,5},{6,7},{1,0},{3,2},{5,4},{7,6},{8,9},{10,11},{12,... | collective-permute-start | bytes 1585160 | tf_op jit(solution)/shard_map/ppermute | solution.py:314
  19.7 6.2 %collective-permute-start.6 = (f32[128,128]{1,0:T(8,128)S(1)}, f32[128,128]{1,0:T(8,128)S(1)}, u32[]{:S(2)}, u32[]{:S(2)}) collective-permute-start(f32[128,128]{1,0:T(8,128)S(1)} %get-tuple-element.36.xa), channel_id=1, source_target_pairs={{0,32},{64,96},{32,0},{96,64},{1,33},{65,97},{33,1},{97,65},{2,34}... | collective-permute-start | bytes 196616 | tf_op jit(solution)/shard_map/ppermute | solution.py:314
  22.2 9.8 %collective-permute-start.7 = (f32[128,128]{1,0:T(8,128)S(1)}, f32[128,128]{1,0:T(8,128)S(1)}, u32[]{:S(2)}, u32[]{:S(2)}) collective-permute-start(f32[128,128]{1,0:T(8,128)S(1)} %get-tuple-element.37.xb), channel_id=1, source_target_pairs={{32,64},{64,32},{33,65},{65,33},{34,66},{66,34},{35,67},{67,35},{3... | collective-permute-start | bytes 196616 | tf_op jit(solution)/shard_map/ppermute | solution.py:314
  25.8 6.2 %collective-permute-start.4 = (f32[512,128]{1,0:T(8,128)S(1)}, f32[512,128]{1,0:T(8,128)S(1)}, u32[]{:S(2)}, u32[]{:S(2)}) collective-permute-start(f32[512,128]{1,0:T(8,128)S(1)} %get-tuple-element.34.yea), channel_id=1, source_target_pairs={{0,8},{16,24},{8,0},{24,16},{1,9},{17,25},{9,1},{25,17},{2,10},{18... | collective-permute-start | bytes 786440 | tf_op jit(solution)/shard_map/ppermute | solution.py:314
  25.9 8.0 %collective-permute-start.5 = (f32[512,128]{1,0:T(8,128)S(1)}, f32[512,128]{1,0:T(8,128)S(1)}, u32[]{:S(2)}, u32[]{:S(2)}) collective-permute-start(f32[512,128]{1,0:T(8,128)S(1)} %get-tuple-element.35.yeb), channel_id=1, source_target_pairs={{8,16},{16,8},{9,17},{17,9},{10,18},{18,10},{11,19},{19,11},{12,20... | collective-permute-start | bytes 786440 | tf_op jit(solution)/shard_map/ppermute | solution.py:314

commit v4 on v3

--- a/solution.py
+++ b/solution.py
@@ -117,7 +117,7 @@
         )
         for pan in range(panels)
     ]
-    for copy in lcopies[:2]:
+    for copy in lcopies:
         copy.start()
     fetch.wait()
     at = positions(osmem)
@@ -131,8 +131,6 @@
             for n, k in enumerate(COLUMNS[:4])
         ]
         ccopies.append(group)
-        if pan >= 2:
-            lcopies[pan].start()
         for copy in group:
             copy.start()
     scopies = stiff_copies(at, stiff, sbuf, ssem, EDGE_BLOCKS)
@@ -149,7 +147,7 @@
         lcopies[pan].wait()
         for copy in ccopies[pan]:
             copy.wait()
-        if pan == 2:
+        if pan == 0:
             for copy in later:
                 copy.start()
         wbd[pan * PAN : (pan + 1) * PAN, :] = weigh(lbuf, cbuf, slice(0, 512), pan)
@@ -201,9 +199,10 @@
     r, c = rows_ge()
     above = r <= c
     row = lax.broadcasted_iota(jnp.int32, (8, BLK), 0) == 1
-    za_out[slot(7)] = za_out[slot(7)] + jnp.where(above, fya[:BLK], fyb[:BLK])
-    za_out[FACES:] = za_out[FACES:] + jnp.where(row, fyb[BLK : BLK + 1], 0.0)
-    zb_out[slot(7)] = zb_out[slot(7)] + jnp.where(above, fyb[:BLK], fya[:BLK])
+    below, diagonal = known("gy", fyb[:BLK]), known("gy", fyb[BLK : BLK + 1])
+    za_out[slot(7)] = za_out[slot(7)] + jnp.where(above, fya[:BLK], below)
+    za_out[FACES:] = za_out[FACES:] + jnp.where(row, diagonal, 0.0)
+    zb_out[slot(7)] = zb_out[slot(7)] + jnp.where(above, below, fya[:BLK])
     zb_out[FACES:] = zb_out[FACES:] + jnp.where(row, fya[BLK : BLK + 1], 0.0)
 
 
@@ -290,28 +289,47 @@
 def last_kernel(order, za, zb, fza, fzb, yea, yeb, fyea, fyeb, xa, xb, fxa, fxb, before, out, osmem, stage, osem, wsem):
     del before
     writer = Writer(order, osmem, osem, out, stage, wsem)
-    for pairs, packs, own, other in ((Z_LOW, Z_LOW_PACK, zb, fzb), (Z_HIGH, Z_HIGH_PACK, za, fza)):
+    for pairs, packs, own, other, take in (
+        (Z_LOW, Z_LOW_PACK, zb, fzb, lambda value: known("gz", value)),
+        (Z_HIGH, Z_HIGH_PACK, za, fza, lambda value: value),
+    ):
         for n, (k, l) in enumerate(pairs):
-            writer.emit(k, l, own[slot(n)] + other[slot(n)])
+            writer.emit(k, l, own[slot(n)] + take(other[slot(n)]))
         for n, (k, l) in enumerate(packs):
             row = slice(FACES + n, FACES + n + 1)
-            first, second = unpack(own[slot(6 + n)] + other[slot(6 + n)], own[row] + other[row])
+            first, second = unpack(own[slot(6 + n)] + take(other[slot(6 + n)]), own[row] + take(other[row]))
             writer.emit(k, k, first)
             writer.emit(l, l, second)
         if writer.at is None:
             writer.ready()
-    for pairs, own, other in ((Y_HIGH, yea, fyea), (Y_LOW, yeb, fyeb)):
-        for n, (k, l) in enumerate(pairs):
-            writer.emit(k, l, own[slot(n)] + other[slot(n)])
-    writer.emit(0, 0, xb[...] + fxb[...])
+    for n, (k, l) in enumerate(Y_HIGH):
+        writer.emit(k, l, yea[slot(n)] + fyea[slot(n)])
+    for n, (k, l) in enumerate(Y_LOW):
+        writer.emit(k, l, yeb[slot(n)] + known("gy", fyeb[slot(n)]))
+    writer.emit(0, 0, xb[...] + known("gx", fxb[...]))
     writer.emit(1, 1, xa[...] + fxa[...])
     writer.finish()
 
 
-def exchange(value, axis, start):
-    size = lax.axis_size(axis)
-    pairs = [(i, i + 1) for i in range(start, size - 1, 2)]
-    return lax.ppermute(value, axis, pairs + [(j, i) for i, j in pairs])
+def exchange_high(value, axis):
+    return lax.ppermute(value, axis, [(i, i ^ 1) for i in range(lax.axis_size(axis))])
+
+
+def exchange_low(value, axis):
+    size, across = lax.axis_size(axis), lax.axis_size("gx")
+    if axis == "gx":
+        return lax.ppermute(value, axis, [(i, size - 1 - i) for i in range(size)])
+    pairs = []
+    for x in range(across):
+        for i in range(size):
+            to = (x ^ 1, i) if i in (0, size - 1) else (x, ((i - 1) ^ 1) + 1)
+            pairs.append((x * size + i, to[0] * size + to[1]))
+    return lax.ppermute(value, ("gx", axis), pairs)
+
+
+def known(axis, value):
+    at = lax.axis_index(axis)
+    return jnp.where((at > 0) & (at < lax.axis_size(axis) - 1), value, 0.0)
 
 
 HBM = pl.BlockSpec(memory_space=pltpu.HBM)
@@ -366,8 +384,8 @@
         cost_estimate=cost(3, 8),
         name="edges",
     )(order, inverse, coupled, stiff)
-    fya = exchange(yda, "gy", 0)
-    fyb = exchange(ydb, "gy", 1)
+    fya = exchange_high(yda, "gy")
+    fyb = exchange_low(ydb, "gy")
     wac, za, zb = pl.pallas_call(
         face_kernel,
         out_shape=(shape(rows, 512, dtype=half), shape(MESSAGE, BLK), shape(MESSAGE, BLK)),
@@ -387,8 +405,8 @@
         cost_estimate=cost(0.1, 0.1),
         name="join",
     )(za, zb, fya, fyb)
-    fzb = exchange(zb, "gz", 1)
-    fza = exchange(za, "gz", 0)
+    fzb = exchange_low(zb, "gz")
+    fza = exchange_high(za, "gz")
     wef, yea, yeb, xa, xb, keep = pl.pallas_call(
         side_kernel,
         out_shape=(
@@ -405,10 +423,10 @@
         cost_estimate=cost(3, 1),
         name="sides",
     )(sall, lbuf, cbuf, wbd, za)
-    fyea = exchange(yea, "gy", 0)
-    fyeb = exchange(yeb, "gy", 1)
-    fxa = exchange(xa, "gx", 0)
-    fxb = exchange(xb, "gx", 1)
+    fyea = exchange_high(yea, "gy")
+    fyeb = exchange_low(yeb, "gy")
+    fxa = exchange_high(xa, "gx")
+    fxb = exchange_low(xb, "gx")
     out = pl.pallas_call(
         rest_kernel,
         out_shape=shape(size, size),

time: 36.5 us -> 31.9 us (0.87)
  starting transfers between devices: 16.8 us -> 8.84 us
  waiting for transfers between devices: 2.64 us -> 5.78 us
    ppermute x8, starting transfers between devices: 16.8 us -> 8.84 us  [the longest x3 3.79 us: exchange_low(): return lax.ppermute(value, ('gx', axis), pairs)]
    ppermute x8, waiting for transfers between devices: 2.64 us -> 5.78 us  [the longest x1 4.77 us: exchange_low(): return lax.ppermute(value, axis, [(i, size - 1 - i) for i in range(size)])]
  transfers between devices with their start and end apart: 8 -> 8, of which waited for: 3 -> 2; matrix products, arithmetic and copies ran while one was open for 0% -> 0% of each run, Pallas kernels for 25% -> 29%
where the time goes in v4:
time: 31.9 us; the launch traced here: 31.5 us
  Pallas kernels  16.8 us (53%)
  starting transfers between devices  8.84 us (28%)
  waiting for transfers between devices  5.78 us (18%)
    pallas_call x1, Pallas kernels, shards(): pl.pallas_call(edge_kernel, out_shape=(shape(rows, rows, dtype=half), sha...  5.13 us
    ppermute x1, waiting for transfers between devices, exchange_low(): return lax.ppermute(value, axis, [(i, size - 1 - i) for i in range(size)])  4.77 us
    pallas_call x1, Pallas kernels, shards(): pl.pallas_call(rest_kernel, out_shape=shape(size, size), in_specs=[HBM] +...  4.07 us
    ppermute x3, starting transfers between devices, exchange_low(): return lax.ppermute(value, ('gx', axis), pairs)  3.79 us
    ppermute x4, starting transfers between devices, exchange_high(): lax.ppermute(value, axis, [(i, i ^ 1) for i in range(lax.axis_size(axis))])  3.26 us
    pallas_call x1, Pallas kernels, shards(): pl.pallas_call(side_kernel, out_shape=(shape(rows, 512, dtype=half), shap...  2.65 us
    pallas_call x1, Pallas kernels, shards(): pl.pallas_call(last_kernel, out_shape=shape(size, size), in_specs=[HBM] +...  2.46 us
    pallas_call x1, Pallas kernels, shards(): pl.pallas_call(face_kernel, out_shape=(shape(rows, 512, dtype=half), shap...  2.44 us
  transfers between devices with their start and end apart: 8, of which 2 were waited for; matrix products, arithmetic and copies ran while one was open for 0% of the time, Pallas kernels for 29%

profile of v4, /device:TPU:21, one launch (start us, length us, event | category | flops | bytes accessed | tf_op | source)
XLA Modules:
  0.0 31.5 jit_solution(779662592364537301)
XLA Ops:
  0.0 5.1 %edges.1 = (bf16[1536,1536]{1,0:T(8,128)(2,1)S(1)}, bf16[1536,1536]{1,0:T(8,128)(2,1)S(1)}, bf16[9216,128]{1,0:T(8,128)(2,1)S(1)}, bf16[1536,512]{1,0:T(8,128)(2...) custom-call(s32[12]{0:T(128)} %bitcast.8, bf16[1536,1536]{1,0:T(8,128)(2,1)} %bitcast.5, ...), custom_call_target="tpu_custom_call" | custom-call | flops 3000000000 | bytes 8000000 | tf_op jit(solution)/shard_map/edges/pallas_call | solution.py:369
  5.1 1.1 %collective-permute-start = (f32[136,128]{1,0:T(8,128)S(1)}, f32[136,128]{1,0:T(8,128)S(1)}, u32[]{:S(2)}, u32[]{:S(2)}) collective-permute-start(f32[136,128]{1,0:T(8,128)S(1)} %get-tuple-element.30), channel_id=1, source_target_pairs={{0,8},{8,0},{16,24},{24,16},{1,9},{9,1},{17,25},{25,17},{2,10},{10... | collective-permute-start | bytes 208904 | tf_op jit(solution)/shard_map/ppermute | solution.py:315
  6.2 0.0 collective-permute-start.1
  6.2 2.4 %faces.1 = (bf16[1536,512]{1,0:T(8,128)(2,1)S(1)}, f32[1032,128]{1,0:T(8,128)S(1)}, f32[1032,128]{1,0:T(8,128)S(1)}) custom-call(bf16[9216,128]{1,0:T(8,128)(2,1)S(1)} %get-tuple-element.23.sall, bf16[1536,1536]{1,0:T(8,128)(2,1)S(1)} %get-tuple-element.24.lbuf, bf16[1536,1536]{1,0:T(8,128)(2,1)S(1)} %get-tuple-element.25.cbuf, ...), custom_call_target="tpu_custom_call" | custom-call | flops 3000000000 | bytes 1000000 | tf_op jit(solution)/shard_map/faces/pallas_call | solution.py:389
  8.7 0.0 collective-permute-done.fya
  8.7 1.0 %collective-permute-done.1.fyb = f32[136,128]{1,0:T(8,128)S(1)} collective-permute-done((f32[136,128]{1,0:T(8,128)S(1)}, f32[136,128]{1,0:T(8,128)S(1)}, u32[]{:S(2)}, u32[]{:S(2)}) %collective-permute-start.1) | collective-permute-done | bytes 69664 | tf_op jit(solution)/shard_map/ppermute | solution.py:327
  9.7 3.8 %collective-permute-start.3 = (f32[1032,128]{1,0:T(8,128)S(1)}, f32[1032,128]{1,0:T(8,128)S(1)}, u32[]{:S(2)}, u32[]{:S(2)}) collective-permute-start(f32[1032,128]{1,0:T(8,128)S(1)} %get-tuple-element.33.zb), channel_id=1, source_target_pairs={{0,32},{1,2},{2,1},{3,4},{4,3},{5,6},{6,5},{7,39},{32,0},{33,34},{... | collective-permute-start | bytes 1585160 | tf_op jit(solution)/shard_map/ppermute | solution.py:327
  13.5 0.0 collective-permute-start.2
  13.5 2.7 %sides.1 = (bf16[1536,512]{1,0:T(8,128)(2,1)S(1)}, f32[512,128]{1,0:T(8,128)S(1)}, f32[512,128]{1,0:T(8,128)S(1)}, f32[128,128]{1,0:T(8,128)S(1)}, f32[128,128]{1,0:T(8,128)S(1)}, /*index=5*/f32[1024,128]{1,0:T(8,128)S(1)}) custom-call(bf16[9216,128]{1,0:T(8,128)(2,1)S(1)} %get-tuple-element.23.sall, bf16[1536,1536]{1,0:T(8,128)(2,1)S(1)} %get-tuple-element.24.lbuf, ...), custom_call_target="tpu_custom_call" | custom-call | flops 3000000000 | bytes 1000000 | tf_op jit(solution)/shard_map/sides/pallas_call | solution.py:410
  16.2 2.2 %collective-permute-start.6 = (f32[128,128]{1,0:T(8,128)S(1)}, f32[128,128]{1,0:T(8,128)S(1)}, u32[]{:S(2)}, u32[]{:S(2)}) collective-permute-start(f32[128,128]{1,0:T(8,128)S(1)} %get-tuple-element.36.xa), channel_id=1, source_target_pairs={{0,32},{32,0},{64,96},{96,64},{1,33},{33,1},{65,97},{97,65},{2,34}... | collective-permute-start | bytes 196616 | tf_op jit(solution)/shard_map/ppermute | solution.py:315
  18.3 1.8 %collective-permute-start.7 = (f32[128,128]{1,0:T(8,128)S(1)}, f32[128,128]{1,0:T(8,128)S(1)}, u32[]{:S(2)}, u32[]{:S(2)}) collective-permute-start(f32[128,128]{1,0:T(8,128)S(1)} %get-tuple-element.37.xb), channel_id=1, source_target_pairs={{0,96},{32,64},{64,32},{96,0},{1,97},{33,65},{65,33},{97,1},{2,98}... | collective-permute-start | bytes 196616 | tf_op jit(solution)/shard_map/ppermute | solution.py:321
  20.1 0.0 collective-permute-start.4
  20.1 0.0 collective-permute-done.6.fxa
  20.1 0.0 collective-permute-start.5
  20.1 4.1 %rest.1.before = f32[1536,1536]{1,0:T(8,128)} custom-call(s32[12]{0:T(128)} %bitcast.9, bf16[9216,128]{1,0:T(8,128)(2,1)S(1)} %get-tuple-element.23.sall, bf16[1536,512]{1,0:T(8,128)(2,1)S(1)} %get-tuple-element.26.wbd, bf16[1536,512]{1,0:T(8,128)(2,1)S(1)} %get-tuple-element.38.wac, bf16[1536,512]{1,0:T(8,128)(2,1)S(1)} %get-tuple-element.39.wef, ...), custom_call_target="tpu_custom_call" | custom-call | flops 3000000000 | bytes 8000000 | tf_op jit(solution)/shard_map/rest/pallas_call | solution.py:430
  24.2 4.8 %collective-permute-done.7.fxb = f32[128,128]{1,0:T(8,128)S(1)} collective-permute-done((f32[128,128]{1,0:T(8,128)S(1)}, f32[128,128]{1,0:T(8,128)S(1)}, u32[]{:S(2)}, u32[]{:S(2)}) %collective-permute-start.7) | collective-permute-done | bytes 65568 | tf_op jit(solution)/shard_map/ppermute | solution.py:321
  29.0 0.0 collective-permute-done.4.fyea
  29.0 0.0 collective-permute-done.5.fyeb
  29.0 0.0 collective-permute-done.3.fzb
  29.0 0.0 collective-permute-done.2.fza
  29.0 2.5 %last.1 = f32[1536,1536]{1,0:T(8,128)} custom-call(s32[12]{0:T(128)} %bitcast.10, f32[1032,128]{1,0:T(8,128)S(1)} %get-tuple-element.32.after.za, f32[1032,128]{1,0:T(8,128)S(1)} %get-tuple-element.33.zb, f32[1032,128]{1,0:T(8,128)S(1)} %collective-permute-done.2.fza, f32[1032,128]{1,0:T(8,128)S(1)} %collective-permute-done.3.fzb, ...), custom_call_target="tpu_custom_call", output_to_operand_aliasing={{}: (13, {})} | custom-call | flops 100000000 | bytes 3000000 | tf_op jit(solution)/shard_map/last/pallas_call | solution.py:446
  (1 shorter events, 0.0 us)
Async XLA Ops:
  5.1 3.5 %collective-permute-start = (f32[136,128]{1,0:T(8,128)S(1)}, f32[136,128]{1,0:T(8,128)S(1)}, u32[]{:S(2)}, u32[]{:S(2)}) collective-permute-start(f32[136,128]{1,0:T(8,128)S(1)} %get-tuple-element.30), channel_id=1, source_target_pairs={{0,8},{8,0},{16,24},{24,16},{1,9},{9,1},{17,25},{25,17},{2,10},{10... | collective-permute-start | bytes 208904 | tf_op jit(solution)/shard_map/ppermute | solution.py:315
  6.2 3.5 %collective-permute-start.1 = (f32[136,128]{1,0:T(8,128)S(1)}, f32[136,128]{1,0:T(8,128)S(1)}, u32[]{:S(2)}, u32[]{:S(2)}) collective-permute-start(f32[136,128]{1,0:T(8,128)S(1)} %get-tuple-element.31), channel_id=1, source_target_pairs={{0,32},{8,16},{16,8},{24,56},{32,0},{40,48},{48,40},{56,24},{64,96... | collective-permute-start | bytes 208904 | tf_op jit(solution)/shard_map/ppermute | solution.py:327
  9.7 19.3 %collective-permute-start.3 = (f32[1032,128]{1,0:T(8,128)S(1)}, f32[1032,128]{1,0:T(8,128)S(1)}, u32[]{:S(2)}, u32[]{:S(2)}) collective-permute-start(f32[1032,128]{1,0:T(8,128)S(1)} %get-tuple-element.33.zb), channel_id=1, source_target_pairs={{0,32},{1,2},{2,1},{3,4},{4,3},{5,6},{6,5},{7,39},{32,0},{33,34},{... | collective-permute-start | bytes 1585160 | tf_op jit(solution)/shard_map/ppermute | solution.py:327
  13.5 15.5 %collective-permute-start.2 = (f32[1032,128]{1,0:T(8,128)S(1)}, f32[1032,128]{1,0:T(8,128)S(1)}, u32[]{:S(2)}, u32[]{:S(2)}) collective-permute-start(f32[1032,128]{1,0:T(8,128)S(1)} %get-tuple-element.32.after.za), channel_id=1, source_target_pairs={{0,1},{1,0},{2,3},{3,2},{4,5},{5,4},{6,7},{7,6},{8,9},{9,8},{10,11... | collective-permute-start | bytes 1585160 | tf_op jit(solution)/shard_map/ppermute | solution.py:315
  16.2 4.0 %collective-permute-start.6 = (f32[128,128]{1,0:T(8,128)S(1)}, f32[128,128]{1,0:T(8,128)S(1)}, u32[]{:S(2)}, u32[]{:S(2)}) collective-permute-start(f32[128,128]{1,0:T(8,128)S(1)} %get-tuple-element.36.xa), channel_id=1, source_target_pairs={{0,32},{32,0},{64,96},{96,64},{1,33},{33,1},{65,97},{97,65},{2,34}... | collective-permute-start | bytes 196616 | tf_op jit(solution)/shard_map/ppermute | solution.py:315
  18.3 10.7 %collective-permute-start.7 = (f32[128,128]{1,0:T(8,128)S(1)}, f32[128,128]{1,0:T(8,128)S(1)}, u32[]{:S(2)}, u32[]{:S(2)}) collective-permute-start(f32[128,128]{1,0:T(8,128)S(1)} %get-tuple-element.37.xb), channel_id=1, source_target_pairs={{0,96},{32,64},{64,32},{96,0},{1,97},{33,65},{65,33},{97,1},{2,98}... | collective-permute-start | bytes 196616 | tf_op jit(solution)/shard_map/ppermute | solution.py:321
  20.1 8.9 %collective-permute-start.4 = (f32[512,128]{1,0:T(8,128)S(1)}, f32[512,128]{1,0:T(8,128)S(1)}, u32[]{:S(2)}, u32[]{:S(2)}) collective-permute-start(f32[512,128]{1,0:T(8,128)S(1)} %get-tuple-element.34.yea), channel_id=1, source_target_pairs={{0,8},{8,0},{16,24},{24,16},{1,9},{9,1},{17,25},{25,17},{2,10},{10... | collective-permute-start | bytes 786440 | tf_op jit(solution)/shard_map/ppermute | solution.py:315
  20.1 8.9 %collective-permute-start.5 = (f32[512,128]{1,0:T(8,128)S(1)}, f32[512,128]{1,0:T(8,128)S(1)}, u32[]{:S(2)}, u32[]{:S(2)}) collective-permute-start(f32[512,128]{1,0:T(8,128)S(1)} %get-tuple-element.35.yeb), channel_id=1, source_target_pairs={{0,32},{8,16},{16,8},{24,56},{32,0},{40,48},{48,40},{56,24},{64,96... | collective-permute-start | bytes 786440 | tf_op jit(solution)/shard_map/ppermute | solution.py:327
